TPU v7x, 128 devices: a whole 4x4x4 slice. The times are simulated.
128 devices in a mesh: lat: 4 (over x_hi, core), lon: 4 (over z), lev: 8 (over y, x_lo).
Axes of the slice: x: 4 (x_hi: 2, x_lo: 2; x = x_hi * 2 + x_lo), y: 4, z: 4, core: 2. Of those that a mesh axis runs over, the one named last changes fastest.
Arguments:
- initial_heat: float32 [128, 512, 32, 128], P('lat', 'lon', 'lev'), may hold values from 0.5 to 2
- diffusivity_ratio: float32 [128, 512, 32, 128], P('lat', 'lon', 'lev'), may hold values from 0.03 to 0.15
- forcing_term: float32 [128, 512, 32, 128], P('lat', 'lon', 'lev'), may hold values from -0.2 to 0.2
Outputs:
- standard_deviation_score: float32 [128, 512, 32, 128], P('lat', 'lon', 'lev')
- temperature_end: float32 [128, 512, 32, 128], P('lat', 'lon', 'lev')
All inputs are finite; a program needn't handle non-finite values.
Results may differ from a plain program's by a relative error of at most 0.00002.
Values sent between devices are 32-bit elements; how exact they have to be, the bound alone decides.
No kernel may reach another device: no remote copies, remote signals or barrier semaphores. Data moves between devices by JAX's collectives and lax.ppermute only.
A program may use at most 128 MiB of HBM per device.

v0:
```python
import jax
import jax.numpy as jnp
from jax import lax
from jax.sharding import PartitionSpec as P

STEPS = 4


def padded(x, sides, width):
    edges = {}
    for axis, dim in sides:
        size, length = (lax.axis_size(axis), x.shape[dim])
        up = [(i, (i + 1) % size) for i in range(size)]
        last = lax.slice_in_dim(x, length - width, length, axis=dim)
        first = lax.slice_in_dim(x, 0, width, axis=dim)
        edges[dim] = (
            lax.ppermute(last, axis, up),
            lax.ppermute(first, axis, [(b, a) for a, b in up]),
        )
    done = []
    for _, dim in sides:
        low, high = edges[dim]
        around = [(width, width) if d in done else (0, 0) for d in range(x.ndim)]
        x = jnp.concatenate([jnp.pad(low, around), x, jnp.pad(high, around)], axis=dim)
        done.append(dim)
    return x


def sent_to_all(x, axis):
    copies = jnp.broadcast_to(x, (lax.axis_size(axis), *x.shape))
    return lax.all_to_all(copies, axis, split_axis=0, concat_axis=0, tiled=True)


def taken_together(x, axis):
    everything = sent_to_all(x, axis)
    return jnp.sum(everything, axis=0)


def packed_total(arrays, axis):
    ends = [0]
    for a in arrays:
        ends.append(ends[-1] + a.size)
    so_far = taken_together(jnp.concatenate([a.ravel() for a in arrays]), axis)
    return tuple((so_far[b:e].reshape(a.shape) for a, b, e in zip(arrays, ends, ends[1:])))


def without_rim(values, dims):
    for dim in dims:
        values = lax.slice_in_dim(values, 1, values.shape[dim] - 1, axis=dim)
    return values


def shifted_cells(values, dim, start, dims):
    others = [other for other in dims if other != dim]
    values = without_rim(values, others)
    return lax.slice_in_dim(values, start, start + values.shape[dim] - 2, axis=dim)


def march_forward(extended_grid_state, diffusivity_ratio, forcing_term):
    middle = without_rim(extended_grid_state, (0, 1, 2))
    lower = [shifted_cells(extended_grid_state, dim, 0, (0, 1, 2)) for dim in (0, 1, 2)]
    upper = [shifted_cells(extended_grid_state, dim, 2, (0, 1, 2)) for dim in (0, 1, 2)]
    spread = lower[0] + upper[0] + lower[1] + upper[1] + lower[2] + upper[2] - 6.0 * middle
    return middle + diffusivity_ratio * spread + forcing_term


def local(initial_heat, diffusivity_ratio, forcing_term):
    for step in range(STEPS):
        extended_grid_state = padded(initial_heat, (("lat", 0), ("lon", 1), ("lev", 2)), 1)
        initial_heat = march_forward(extended_grid_state, diffusivity_ratio, forcing_term)
    number_of_entries = initial_heat.shape[1] * lax.axis_size("lon")
    guess = 1.0
    moved = initial_heat - guess
    totals, squares = packed_total(
        (jnp.sum(moved, axis=1, keepdims=True), jnp.sum(moved * moved, axis=1, keepdims=True)),
        "lon",
    )
    row_mean_estimate = guess + totals / number_of_entries
    deviations_from_mean = initial_heat - row_mean_estimate
    line_variance = squares / number_of_entries - totals / number_of_entries * (
        totals / number_of_entries
    )
    standard_deviation_score = deviations_from_mean * lax.rsqrt(line_variance + 0.0001)
    return (standard_deviation_score, initial_heat)


def solution(mesh):
    placed = (
        P("lat", "lon", "lev", None),
        P("lat", "lon", "lev", None),
        P("lat", "lon", "lev", None),
    )
    return jax.shard_map(
        local,
        mesh=mesh,
        in_specs=placed,
        out_specs=(P("lat", "lon", "lev", None), P("lat", "lon", "lev", None)),
        check_vma=False,
    )
```

profile of v0, /device:TPU:1, one launch (start us, length us, event | category | flops | bytes accessed | tf_op | source)
XLA Modules:
  0.0 598.0 jit_solution(13675427221701031850)
XLA Ops:
  0.6 4.7 copy.58
  5.8 2.1 collective-permute-start.4
  7.9 2.5 collective-permute-start.5
  10.5 3.8 collective-permute-start
  14.3 1.7 collective-permute-start.2
  16.0 2.2 collective-permute-start.3
  18.2 2.0 collective-permute-done.2
  20.3 82.4 %collective-permute-done = f32[1,128,4,128]{3,1,2,0:T(8,128)S(1)} collective-permute-done((f32[1,128,4,128]{3,1,2,0:T(8,128)S(1)}, f32[1,128,4,128]{3,1,2,0:T(8,128)S(1)}, u32[]{:S(2)}, u32[]{:S(2)}) %collective-permute-start) | collective-permute-done | bytes 262176 | tf_op jit(solution)/shard_map/ppermute | solution.py:17
  103.5 8.4 %constant_dynamic-update-slice_fusion.1 = f32[34,128,4,128]{3,1,2,0:T(8,128)} fusion(f32[34,128,4,128]{3,1,2,0:T(8,128)} %constant_dynamic-update-slice_fusion.2, f32[32,128,4,128]{3,2,1,0:T(4,128)} %param.3), kind=kLoop, calls=%fused_computation.121 | loop fusion | bytes 16777216
  112.7 30.7 %fusion.38 = f32[32,128,4,128]{3,1,2,0:T(8,128)} fusion(f32[32,128,4,128]{3,1,2,0:T(8,128)} %copy-done, f32[32,128,1,128]{3,1,2,0:T(8,128)} %collective-permute-done.5, f32[34,1,4,128]{3,1,2,0:T(1,128)S(1)} %pad.51, f32[34,128,4,128]{3,1,2,0:T(8,128)} %constant_dynamic-update-slice_fusion, f32[34,1,4,128]{3,1,2,0:T(1,128)S(1)} %pad.50, ...), kind=kLoop, calls=%fused_computation.93 | loop fusion | flops 54525952 | bytes 47325184 | tf_op jit(solution)/shard_map/add | solution.py:64
  143.4 2.5 fusion.55
  145.9 1.3 collective-permute-start.10
  147.3 2.3 collective-permute-start.11
  150.6 4.6 collective-permute-start.6
  155.3 1.3 fusion.57
  156.6 1.7 collective-permute-start.8
  158.3 4.1 collective-permute-done.8
  162.4 1.7 collective-permute-start.9
  164.1 1.9 collective-permute-done.9
  166.0 73.5 %collective-permute-done.6 = f32[1,128,4,128]{3,1,2,0:T(8,128)S(1)} collective-permute-done((f32[1,128,4,128]{3,1,2,0:T(8,128)S(1)}, f32[1,128,4,128]{3,1,2,0:T(8,128)S(1)}, u32[]{:S(2)}, u32[]{:S(2)}) %collective-permute-start.6) | collective-permute-done | bytes 262176 | tf_op jit(solution)/shard_map/ppermute | solution.py:17
  239.5 6.9 %collective-permute-done.7 = f32[1,128,4,128]{3,1,2,0:T(8,128)S(1)} collective-permute-done((f32[1,128,4,128]{3,1,2,0:T(8,128)S(1)}, f32[1,128,4,128]{3,1,2,0:T(8,128)S(1)}, u32[]{:S(2)}, u32[]{:S(2)}) %collective-permute-start.7) | collective-permute-done | bytes 262176 | tf_op jit(solution)/shard_map/ppermute | solution.py:18
  246.5 1.3 copy-done.1
  247.8 33.3 %fusion.27 = f32[32,128,4,128]{3,1,2,0:T(8,128)} fusion(f32[32,128,4,128]{3,1,2,0:T(8,128)} %fusion.38, f32[32,128,1,128]{3,1,2,0:T(8,128)} %collective-permute-done.11, f32[34,1,4,128]{3,1,2,0:T(1,128)S(1)} %pad.55, f32[34,1,4,128]{3,1,2,0:T(1,128)S(1)} %pad.54, f32[1,128,4,128]{3,1,2,0:T(8,128)S(1)} %collective-permute-done.7, ...), kind=kLoop, calls=%fused_computation.64 | loop fusion | flops 71303168 | bytes 38412288 | tf_op jit(solution)/shard_map/add | solution.py:64
  281.1 2.5 fusion.52
  284.0 3.3 collective-permute-start.17
  290.3 1.7 collective-permute-start.14
  292.0 4.1 collective-permute-done.14
  296.0 1.5 collective-permute-start.15
  297.5 1.9 collective-permute-done.15
  299.5 79.6 %collective-permute-done.12 = f32[1,128,4,128]{3,1,2,0:T(8,128)S(1)} collective-permute-done((f32[1,128,4,128]{3,1,2,0:T(8,128)S(1)}, f32[1,128,4,128]{3,1,2,0:T(8,128)S(1)}, u32[]{:S(2)}, u32[]{:S(2)}) %collective-permute-start.12) | collective-permute-done | bytes 262176 | tf_op jit(solution)/shard_map/ppermute | solution.py:17
  379.1 2.0 collective-permute-done.13
  381.1 1.3 copy-done.2
  382.4 33.5 %fusion.16 = f32[32,128,4,128]{3,1,2,0:T(8,128)} fusion(f32[32,128,4,128]{3,1,2,0:T(8,128)} %fusion.27, f32[32,128,1,128]{3,1,2,0:T(8,128)} %collective-permute-done.17, f32[34,1,4,128]{3,1,2,0:T(1,128)S(1)} %pad.59, f32[34,1,4,128]{3,1,2,0:T(1,128)S(1)} %pad.58, f32[1,128,4,128]{3,1,2,0:T(8,128)S(1)} %collective-permute-done.13, ...), kind=kLoop, calls=%fused_computation.35 | loop fusion | flops 71303168 | bytes 38412288 | tf_op jit(solution)/shard_map/add | solution.py:64
  415.9 2.5 fusion.49
  418.4 1.4 collective-permute-start.22
  419.7 2.7 collective-permute-start.23
  423.5 2.6 collective-permute-start.18
  427.4 1.7 collective-permute-start.20
  429.1 4.1 collective-permute-done.20
  433.2 1.5 collective-permute-start.21
  434.8 1.9 collective-permute-done.21
  436.7 78.2 %collective-permute-done.18 = f32[1,128,4,128]{3,1,2,0:T(8,128)S(1)} collective-permute-done((f32[1,128,4,128]{3,1,2,0:T(8,128)S(1)}, f32[1,128,4,128]{3,1,2,0:T(8,128)S(1)}, u32[]{:S(2)}, u32[]{:S(2)}) %collective-permute-start.18) | collective-permute-done | bytes 262176 | tf_op jit(solution)/shard_map/ppermute | solution.py:17
  514.9 2.9 collective-permute-done.19
  517.8 36.4 %add_reduce_fusion = (f32[32,4,128]{2,1,0:T(4,128)S(1)}, f32[32,4,128]{2,1,0:T(4,128)S(1)}, f32[32,128,4,128]{3,1,2,0:T(8,128)}) fusion(f32[32,128,4,128]{3,2,1,0:T(4,128)} %param.5, f32[32,128,4,128]{3,1,2,0:T(8,128)} %fusion.16, f32[32,128,1,128]{3,1,2,0:T(8,128)S(1)} %collective-permute-done.23, f32[34,1,4,128]{3,1,2,0:T(1,128)S(1)} %pad.63, ...), kind=kLoop, calls=%fused_computation.112 | loop fusion | flops 79659008 | bytes 38543360 | tf_op jit(solution)/shard_map/reduce_sum | solution.py:75
  555.3 5.2 all-to-all-start
  560.5 14.0 %copy.68 = f32[32,128,4,128]{3,2,1,0:T(4,128)} copy(f32[32,128,4,128]{3,1,2,0:T(8,128)} %get-tuple-element.10) | data formatting | bytes 16777216
  575.0 8.7 %subtract_multiply_fusion = f32[32,128,4,128]{3,1,2,0:T(8,128)} fusion(f32[32,128,4,128]{3,1,2,0:T(8,128)} %get-tuple-element.10, f32[32,4,128]{2,1,0:T(4,128)S(1)} %bitcast.9, f32[32,4,128]{2,1,0:T(4,128)S(1)} %bitcast.8), kind=kLoop, calls=%fused_computation.110 | loop fusion | flops 4194304 | bytes 16908288 | tf_op jit(solution)/shard_map/mul | solution.py:83
  583.6 14.2 %copy.67 = f32[32,128,4,128]{3,2,1,0:T(4,128)} copy(f32[32,128,4,128]{3,1,2,0:T(8,128)} %subtract_multiply_fusion) | data formatting | bytes 16777216
  (48 shorter events, 10.9 us)
Async XLA Ops:
  5.3 106.6 %copy-start = (f32[32,128,4,128]{3,1,2,0:T(8,128)}, f32[32,128,4,128]{3,1,2,0:T(8,128)S(1)}, u32[]{:S(2)}) copy-start(f32[32,128,4,128]{3,1,2,0:T(8,128)S(1)} %copy.58) | copy-start | bytes 25165828
  5.8 106.9 %collective-permute-start.4 = (f32[32,128,1,128]{3,1,2,0:T(8,128)S(1)}, f32[32,128,1,128]{3,1,2,0:T(8,128)}, u32[]{:S(2)}, u32[]{:S(2)}) collective-permute-start(f32[32,128,1,128]{3,1,2,0:T(8,128)S(1)} %get-tuple-element.29), channel_id=1, source_target_pairs={{0,1},{1,2},{2,3},{3,4},{4,5},{5,6},{6,7},{7,0},{8,9},{9,10},{10,1... | collective-permute-start | bytes 6291464 | tf_op jit(solution)/shard_map/ppermute | solution.py:17
  7.9 104.8 %collective-permute-start.5 = (f32[32,128,1,128]{3,1,2,0:T(8,128)S(1)}, f32[32,128,1,128]{3,1,2,0:T(8,128)}, u32[]{:S(2)}, u32[]{:S(2)}) collective-permute-start(f32[32,128,1,128]{3,1,2,0:T(8,128)S(1)} %get-tuple-element.30), channel_id=1, source_target_pairs={{1,0},{2,1},{3,2},{4,3},{5,4},{6,5},{7,6},{0,7},{9,8},{10,9},{11,1... | collective-permute-start | bytes 6291464 | tf_op jit(solution)/shard_map/ppermute | solution.py:18
  10.5 92.3 %collective-permute-start = (f32[1,128,4,128]{3,1,2,0:T(8,128)S(1)}, f32[1,128,4,128]{3,1,2,0:T(8,128)S(1)}, u32[]{:S(2)}, u32[]{:S(2)}) collective-permute-start(f32[1,128,4,128]{3,1,2,0:T(8,128)S(1)} %get-tuple-element.34), channel_id=1, source_target_pairs={{0,32},{32,64},{64,96},{96,0},{1,33},{33,65},{65,97},{97,1},{2,34}... | collective-permute-start | bytes 786440 | tf_op jit(solution)/shard_map/ppermute | solution.py:17
  14.3 5.9 collective-permute-start.2
  16.0 4.2 collective-permute-start.3
  20.2 91.7 %collective-permute-start.1 = (f32[1,128,4,128]{3,1,2,0:T(8,128)S(1)}, f32[1,128,4,128]{3,1,2,0:T(8,128)S(1)}, u32[]{:S(2)}, u32[]{:S(2)}) collective-permute-start(f32[1,128,4,128]{3,1,2,0:T(8,128)S(1)} %get-tuple-element.33), channel_id=1, source_target_pairs={{32,0},{64,32},{96,64},{0,96},{33,1},{65,33},{97,65},{1,97},{34,2}... | collective-permute-start | bytes 786440 | tf_op jit(solution)/shard_map/ppermute | solution.py:18
  102.8 9.9 %slice-start = ((s8[8388608]{0:T(1024)(128)(4,1)}), s8[4194304]{0:T(1024)(128)(4,1)S(1)}, s32[]{:S(2)}) async-start(s8[8388608]{0:T(1024)(128)(4,1)} %bitcast.4), calls=%async_computation.1 | async-start | bytes 8388608
  103.5 9.2 %slice-start.1 = ((s8[8388608]{0:T(1024)(128)(4,1)}), s8[4194304]{0:T(1024)(128)(4,1)S(1)}, s32[]{:S(2)}) async-start(s8[8388608]{0:T(1024)(128)(4,1)} %bitcast.4), calls=%async_computation.2 | async-start | bytes 8388608
  145.9 100.5 %collective-permute-start.10 = (f32[32,128,1,128]{3,1,2,0:T(8,128)S(1)}, f32[32,128,1,128]{3,1,2,0:T(8,128)S(1)}, u32[]{:S(2)}, u32[]{:S(2)}) collective-permute-start(f32[32,128,1,128]{3,1,2,0:T(8,128)S(1)} %get-tuple-element.23), channel_id=1, source_target_pairs={{0,1},{1,2},{2,3},{3,4},{4,5},{5,6},{6,7},{7,0},{8,9},{9,10},{10,1... | collective-permute-start | bytes 6291464 | tf_op jit(solution)/shard_map/ppermute | solution.py:17
  147.3 100.5 %collective-permute-start.11 = (f32[32,128,1,128]{3,1,2,0:T(8,128)S(1)}, f32[32,128,1,128]{3,1,2,0:T(8,128)}, u32[]{:S(2)}, u32[]{:S(2)}) collective-permute-start(f32[32,128,1,128]{3,1,2,0:T(8,128)S(1)} %get-tuple-element.24), channel_id=1, source_target_pairs={{1,0},{2,1},{3,2},{4,3},{5,4},{6,5},{7,6},{0,7},{9,8},{10,9},{11,1... | collective-permute-start | bytes 6291464 | tf_op jit(solution)/shard_map/ppermute | solution.py:18
  150.6 88.9 %collective-permute-start.6 = (f32[1,128,4,128]{3,1,2,0:T(8,128)S(1)}, f32[1,128,4,128]{3,1,2,0:T(8,128)S(1)}, u32[]{:S(2)}, u32[]{:S(2)}) collective-permute-start(f32[1,128,4,128]{3,1,2,0:T(8,128)S(1)} %get-tuple-element.25), channel_id=1, source_target_pairs={{0,32},{32,64},{64,96},{96,0},{1,33},{33,65},{65,97},{97,1},{2,34}... | collective-permute-start | bytes 786440 | tf_op jit(solution)/shard_map/ppermute | solution.py:17
  155.3 91.2 %collective-permute-start.7 = (f32[1,128,4,128]{3,1,2,0:T(8,128)S(1)}, f32[1,128,4,128]{3,1,2,0:T(8,128)S(1)}, u32[]{:S(2)}, u32[]{:S(2)}) collective-permute-start(f32[1,128,4,128]{3,1,2,0:T(8,128)S(1)} %get-tuple-element.26), channel_id=1, source_target_pairs={{32,0},{64,32},{96,64},{0,96},{33,1},{65,33},{97,65},{1,97},{34,2}... | collective-permute-start | bytes 786440 | tf_op jit(solution)/shard_map/ppermute | solution.py:18
  156.6 5.8 collective-permute-start.8
  162.4 3.6 collective-permute-start.9
  246.5 1.3 copy-start.1
  283.6 97.4 %collective-permute-start.16 = (f32[32,128,1,128]{3,1,2,0:T(8,128)S(1)}, f32[32,128,1,128]{3,1,2,0:T(8,128)S(1)}, u32[]{:S(2)}, u32[]{:S(2)}) collective-permute-start(f32[32,128,1,128]{3,1,2,0:T(8,128)S(1)} %get-tuple-element.17), channel_id=1, source_target_pairs={{0,1},{1,2},{2,3},{3,4},{4,5},{5,6},{6,7},{7,0},{8,9},{9,10},{10,1... | collective-permute-start | bytes 6291464 | tf_op jit(solution)/shard_map/ppermute | solution.py:17
  284.0 98.4 %collective-permute-start.17 = (f32[32,128,1,128]{3,1,2,0:T(8,128)S(1)}, f32[32,128,1,128]{3,1,2,0:T(8,128)}, u32[]{:S(2)}, u32[]{:S(2)}) collective-permute-start(f32[32,128,1,128]{3,1,2,0:T(8,128)S(1)} %get-tuple-element.18), channel_id=1, source_target_pairs={{1,0},{2,1},{3,2},{4,3},{5,4},{6,5},{7,6},{0,7},{9,8},{10,9},{11,1... | collective-permute-start | bytes 6291464 | tf_op jit(solution)/shard_map/ppermute | solution.py:18
  288.4 90.7 %collective-permute-start.12 = (f32[1,128,4,128]{3,1,2,0:T(8,128)S(1)}, f32[1,128,4,128]{3,1,2,0:T(8,128)S(1)}, u32[]{:S(2)}, u32[]{:S(2)}) collective-permute-start(f32[1,128,4,128]{3,1,2,0:T(8,128)S(1)} %get-tuple-element.19), channel_id=1, source_target_pairs={{0,32},{32,64},{64,96},{96,0},{1,33},{33,65},{65,97},{97,1},{2,34}... | collective-permute-start | bytes 786440 | tf_op jit(solution)/shard_map/ppermute | solution.py:17
  288.8 92.2 %collective-permute-start.13 = (f32[1,128,4,128]{3,1,2,0:T(8,128)S(1)}, f32[1,128,4,128]{3,1,2,0:T(8,128)S(1)}, u32[]{:S(2)}, u32[]{:S(2)}) collective-permute-start(f32[1,128,4,128]{3,1,2,0:T(8,128)S(1)} %get-tuple-element.20), channel_id=1, source_target_pairs={{32,0},{64,32},{96,64},{0,96},{33,1},{65,33},{97,65},{1,97},{34,2}... | collective-permute-start | bytes 786440 | tf_op jit(solution)/shard_map/ppermute | solution.py:18
  290.3 5.8 collective-permute-start.14
  296.0 3.4 collective-permute-start.15
  381.1 1.3 copy-start.2
  418.4 99.4 %collective-permute-start.22 = (f32[32,128,1,128]{3,1,2,0:T(8,128)S(1)}, f32[32,128,1,128]{3,1,2,0:T(8,128)S(1)}, u32[]{:S(2)}, u32[]{:S(2)}) collective-permute-start(f32[32,128,1,128]{3,1,2,0:T(8,128)S(1)} %get-tuple-element.11), channel_id=1, source_target_pairs={{0,1},{1,2},{2,3},{3,4},{4,5},{5,6},{6,7},{7,0},{8,9},{9,10},{10,1... | collective-permute-start | bytes 6291464 | tf_op jit(solution)/shard_map/ppermute | solution.py:17
  419.7 98.1 %collective-permute-start.23 = (f32[32,128,1,128]{3,1,2,0:T(8,128)S(1)}, f32[32,128,1,128]{3,1,2,0:T(8,128)S(1)}, u32[]{:S(2)}, u32[]{:S(2)}) collective-permute-start(f32[32,128,1,128]{3,1,2,0:T(8,128)S(1)} %get-tuple-element.12), channel_id=1, source_target_pairs={{1,0},{2,1},{3,2},{4,3},{5,4},{6,5},{7,6},{0,7},{9,8},{10,9},{11,1... | collective-permute-start | bytes 6291464 | tf_op jit(solution)/shard_map/ppermute | solution.py:18
  423.5 91.4 %collective-permute-start.18 = (f32[1,128,4,128]{3,1,2,0:T(8,128)S(1)}, f32[1,128,4,128]{3,1,2,0:T(8,128)S(1)}, u32[]{:S(2)}, u32[]{:S(2)}) collective-permute-start(f32[1,128,4,128]{3,1,2,0:T(8,128)S(1)} %get-tuple-element.15), channel_id=1, source_target_pairs={{0,32},{32,64},{64,96},{96,0},{1,33},{33,65},{65,97},{97,1},{2,34}... | collective-permute-start | bytes 786440 | tf_op jit(solution)/shard_map/ppermute | solution.py:17
  426.1 91.7 %collective-permute-start.19 = (f32[1,128,4,128]{3,1,2,0:T(8,128)S(1)}, f32[1,128,4,128]{3,1,2,0:T(8,128)S(1)}, u32[]{:S(2)}, u32[]{:S(2)}) collective-permute-start(f32[1,128,4,128]{3,1,2,0:T(8,128)S(1)} %get-tuple-element.16), channel_id=1, source_target_pairs={{32,0},{64,32},{96,64},{0,96},{33,1},{65,33},{97,65},{1,97},{34,2}... | collective-permute-start | bytes 786440 | tf_op jit(solution)/shard_map/ppermute | solution.py:18
  427.4 5.8 collective-permute-start.20
  433.2 3.4 collective-permute-start.21
  555.3 19.1 %all-to-all-start = ((f32[4,1,32768]{2,1,0:T(1,128)}), f32[4,1,32768]{2,1,0:T(1,128)S(1)}, u32[]{:S(2)}, u32[]{:S(2)}) async-start(f32[4,1,32768]{2,1,0:T(1,128)} %broadcast_in_dim.3), calls=%async_computation | async-start | bytes 1048576 | tf_op jit(solution)/shard_map/all_to_all | solution.py:31
where the time goes:
time: 606 us; the launch traced here: 598 us
  waiting for transfers between devices  345 us (57%)
  other arithmetic  143 us (24%)
  local copies, waits for them, and re-layouts  62 us (10%)
  starting transfers between devices  46.3 us (8%)
    ppermute x12, waiting for transfers between devices, padded(): lax.ppermute(last, axis, up)  328 us
    add x3, other arithmetic, march_forward(): return middle + diffusivity_ratio * spread + forcing_term  97.5 us
    unnamed x15, local copies, waits for them, and re-layouts  44.6 us
    reduce_sum x1, other arithmetic, local(): jnp.sum(moved, axis=1, keepdims=True)  36.4 us
    ppermute x12, starting transfers between devices, padded(): lax.ppermute(last, axis, up)  23.5 us
    ppermute x12, starting transfers between devices, padded(): lax.ppermute(first, axis, [(b, a) for a, b in up])  17.7 us
    ppermute x12, waiting for transfers between devices, padded(): lax.ppermute(first, axis, [(b, a) for a, b in up])  17.5 us
    slice x11, local copies, waits for them, and re-layouts, padded(): last = lax.slice_in_dim(x, length - width, length, axis=dim)  15.2 us
  transfers between devices with their start and end apart: 25, of which 14 were waited for; matrix products, arithmetic and copies ran while one was open for 5% of the time, Pallas kernels for 0%

commit v1 on v0

v1 whole, which is shorter than its diff:
```python
import jax
import jax.numpy as jnp
from jax import lax
from jax.experimental import pallas as pl
from jax.experimental.pallas import tpu as pltpu
from jax.sharding import PartitionSpec as P

STEPS = 4
ROWS = 8


def shift(x, axis, by):
    size = lax.axis_size(axis)
    return lax.ppermute(x, axis, [(i, (i + by) % size) for i in range(size)])


def update_body(last, c, before, after, low, high, d, f, south, north, west, east, *outs):
    i = pl.program_id(0)
    n = pl.num_programs(0)
    out = outs[0]
    width = c.shape[1]
    place = lax.broadcasted_iota(jnp.int32, c.shape[1:], 0)
    first_row = jnp.where(i == 0, south[0], before[0])
    final_row = jnp.where(i == n - 1, north[0], after[0])
    for r in range(ROWS):
        x = c[r]
        lat_low = first_row if r == 0 else c[r - 1]
        lat_high = final_row if r == ROWS - 1 else c[r + 1]
        left = jnp.where(place == 0, west[0, r : r + 1, :], pltpu.roll(x, 1, 0))
        right = jnp.where(place == width - 1, east[0, r : r + 1, :], pltpu.roll(x, width - 1, 0))
        spread = lat_low + lat_high + left + right + low[r] + high[r] - 6.0 * x
        y = x + d[r] * spread + f[r]
        out[r] = y
        if last:
            total = jnp.sum(y, axis=0, keepdims=True)
            away = y - total * (1.0 / width)
            outs[1][r : r + 1, :] = total
            outs[2][r : r + 1, :] = jnp.sum(away * away, axis=0, keepdims=True)


def update(c, low, high, d, f, sides, k, last=False):
    south, north, west, east = sides
    depth, width, lanes = c.shape
    block = pl.BlockSpec((ROWS, width, lanes), lambda i: (i, 0, 0))
    row_before = pl.BlockSpec((1, width, lanes), lambda i: (jnp.maximum(i * ROWS - 1, 0), 0, 0))
    row_after = pl.BlockSpec((1, width, lanes), lambda i: (jnp.minimum(i * ROWS + ROWS, depth - 1), 0, 0))
    lat_edge = pl.BlockSpec((1, width, lanes), lambda i: (k, 0, 0))
    lon_edge = pl.BlockSpec((1, ROWS, lanes), lambda i: (k, i, 0))
    stat = pl.BlockSpec((ROWS, lanes), lambda i: (i, 0))
    shapes = [jax.ShapeDtypeStruct(c.shape, c.dtype)]
    specs = [block]
    if last:
        shapes += [jax.ShapeDtypeStruct((depth, lanes), c.dtype)] * 2
        specs += [stat] * 2
    got = pl.pallas_call(
        lambda *refs: update_body(last, *refs),
        grid=(depth // ROWS,),
        in_specs=[block, row_before, row_after, block, block, block, block, lat_edge, lat_edge, lon_edge, lon_edge],
        out_specs=specs,
        out_shape=shapes,
        compiler_params=pltpu.CompilerParams(vmem_limit_bytes=16 * 2**20),
        cost_estimate=pl.CostEstimate(flops=10 * c.size, bytes_accessed=6 * 4 * c.size, transcendentals=0),
        name="update",
    )(c, c, c, low, high, d, f, south, north, west, east)
    return got if last else got[0]


def sides_of(planes):
    def cut(take):
        return jnp.stack([take(p) for p in planes])

    return (
        shift(cut(lambda p: p[-1]), "lat", 1),
        shift(cut(lambda p: p[0]), "lat", -1),
        shift(cut(lambda p: p[:, -1]), "lon", 1),
        shift(cut(lambda p: p[:, 0]), "lon", -1),
    )


def finish_body(count, *refs):
    planes, stats, (score, end) = refs[:4], refs[4:-2], refs[-2:]
    width = planes[0].shape[1]
    for z in range(4):
        group, k = (0, 0) if z == 0 else (1, z - 1)
        sums = [stats[4 * group + j][k] for j in range(4)]
        powers = [stats[4 * group + j][k + (1 if group == 0 else 3)] for j in range(4)]
        mean = (sums[0] + sums[1] + sums[2] + sums[3]) * (1.0 / count)
        power = powers[0] + powers[1] + powers[2] + powers[3]
        for s in sums:
            gap = s * (1.0 / width) - mean
            power = power + width * (gap * gap)
        scale = lax.rsqrt(power * (1.0 / count) + 0.0001)
        for r in range(ROWS):
            y = planes[z][r]
            end[r, pl.ds(z, width, stride=4), :] = y
            score[r, pl.ds(z, width, stride=4), :] = (y - mean[r : r + 1, :]) * scale[r : r + 1, :]


def finish(planes, edge_stats, inner_stats):
    depth, width, lanes = planes[0].shape
    block = pl.BlockSpec((ROWS, width, lanes), lambda i: (i, 0, 0))
    wide = pl.BlockSpec((ROWS, 4 * width, lanes), lambda i: (i, 0, 0))
    edge = pl.BlockSpec((2, ROWS, lanes), lambda i: (0, i, 0))
    inner = pl.BlockSpec((6, ROWS, lanes), lambda i: (0, i, 0))
    count = width * lax.axis_size("lon")
    full = jax.ShapeDtypeStruct((depth, 4 * width, lanes), planes[0].dtype)
    score, end = pl.pallas_call(
        lambda *refs: finish_body(count, *refs),
        grid=(depth // ROWS,),
        in_specs=[block] * 4 + [edge] * 4 + [inner] * 4,
        out_specs=[wide] * 2,
        out_shape=[full] * 2,
        compiler_params=pltpu.CompilerParams(vmem_limit_bytes=24 * 2**20),
        cost_estimate=pl.CostEstimate(flops=20 * 4 * planes[0].size, bytes_accessed=12 * 4 * planes[0].size, transcendentals=0),
        name="finish",
    )(*planes, *edge_stats, *inner_stats)
    shape = (depth, width, 4, lanes)
    return score.reshape(shape), end.reshape(shape)


def from_all(x):
    return [x] + [shift(x, "lon", by) for by in (1, -1, 2)]


def local(initial_heat, diffusivity_ratio, forcing_term):
    u = [initial_heat[:, :, z, :] for z in range(4)]
    up = shift(u[3], "lev", 1)
    down = shift(u[0], "lev", -1)
    d = [diffusivity_ratio[:, :, z, :] for z in range(4)]
    f = [forcing_term[:, :, z, :] for z in range(4)]
    whole = sides_of(u)
    where = [(whole, z) for z in range(4)]
    for step in range(STEPS):
        last = step == STEPS - 1
        v = [None] * 4
        first, second = (0, 3) if step % 2 == 0 else (3, 0)
        halo = {0: up, 3: down}

        def advance(z):
            low = halo[0] if z == 0 else u[z - 1]
            high = halo[3] if z == 3 else u[z + 1]
            v[z] = update(u[z], low, high, d[z], f[z], *where[z], last=last)

        next_where = [None] * 4
        faces = {}
        advance(first)
        if not last:
            alone = sides_of([v[first]])
            next_where[first] = (alone, 0)
            faces[first] = shift(v[first], "lev", -1 if first == 0 else 1)
        advance(1)
        advance(2)
        advance(second)
        if not last:
            rest = [z for z in range(4) if z != first]
            together = sides_of([v[z] for z in rest])
            for k, z in enumerate(rest):
                next_where[z] = (together, k)
            faces[second] = shift(v[second], "lev", -1 if second == 0 else 1)
            up, down = faces[3], faces[0]
        u, where = v, next_where
    planes = [g[0] for g in u]
    inner = from_all(jnp.stack([u[z][1] for z in (1, 2, 3)] + [u[z][2] for z in (1, 2, 3)]))
    edge = from_all(jnp.stack([u[0][1], u[0][2]]))
    return finish(planes, edge, inner)


def solution(mesh):
    placed = P("lat", "lon", "lev", None)
    return jax.shard_map(
        local,
        mesh=mesh,
        in_specs=(placed,) * 3,
        out_specs=(placed, placed),
        check_vma=False,
    )
```

time: 606 us -> 462 us (0.76)
  other arithmetic: 143 us -> 2.2 us
  waiting for transfers between devices: 345 us -> 273 us
  starting transfers between devices: 46.3 us -> 82.8 us
  Pallas kernels: 0 us -> 24 us
  local copies, waits for them, and re-layouts: 62 us -> 71.7 us
    add x4 -> x0, other arithmetic: 97.6 us -> none  [the longest x3 97.5 us: march_forward(): return middle + diffusivity_ratio * spread + forcing_term]
    ppermute x24 -> x42, waiting for transfers between devices: 345 us -> 273 us  [shift(): return lax.ppermute(x, axis, [(i, (i + by) % size) for i in range(size)])]
    slice x12 -> x28, local copies, waits for them, and re-layouts: 15.3 us -> 59.3 us  [the longest x1 18.9 us: local(): f = [forcing_term[:, :, z, :] for z in range(4)]]
    unnamed x15 -> x5, local copies, waits for them, and re-layouts: 44.6 us -> 2.45 us
    ppermute x24 -> x42, starting transfers between devices: 41.1 us -> 82.8 us  [shift(): return lax.ppermute(x, axis, [(i, (i + by) % size) for i in range(size)])]
    reduce_sum x2 -> x0, other arithmetic: 36.9 us -> none  [the longest x1 36.4 us: local(): jnp.sum(moved, axis=1, keepdims=True)]
    pallas_call x0 -> x15, Pallas kernels: none -> 24 us  [the longest x14 17.5 us: update(): pl.pallas_call(lambda *refs: update_body(last, *refs), grid=(depth // ROW...]
    mul x1 -> x0, other arithmetic: 8.67 us -> none  [local(): deviations_from_mean * lax.rsqrt(line_variance + 0.0001)]
  transfers between devices with their start and end apart: 25 -> 42, of which waited for: 14 -> 16; matrix products, arithmetic and copies ran while one was open for 5% -> 12% of each run, Pallas kernels for 0% -> 4%
where the time goes in v1:
time: 462 us; the launch traced here: 455 us
  waiting for transfers between devices  273 us (59%)
  starting transfers between devices  82.8 us (18%)
  local copies, waits for them, and re-layouts  71.7 us (16%)
  Pallas kernels  24 us (5%)
    ppermute x42, waiting for transfers between devices, shift(): return lax.ppermute(x, axis, [(i, (i + by) % size) for i in range(size)])  273 us
    ppermute x42, starting transfers between devices, shift(): return lax.ppermute(x, axis, [(i, (i + by) % size) for i in range(size)])  82.8 us
    slice x1, local copies, waits for them, and re-layouts, local(): f = [forcing_term[:, :, z, :] for z in range(4)]  18.9 us
    slice x1, local copies, waits for them, and re-layouts, local(): u = [initial_heat[:, :, z, :] for z in range(4)]  18.9 us
    slice x1, local copies, waits for them, and re-layouts, local(): d = [diffusivity_ratio[:, :, z, :] for z in range(4)]  18.8 us
    pallas_call x14, Pallas kernels, update(): pl.pallas_call(lambda *refs: update_body(last, *refs), grid=(depth // ROW...  17.5 us
  transfers between devices with their start and end apart: 42, of which 16 were waited for; matrix products, arithmetic and copies ran while one was open for 12% of the time, Pallas kernels for 4%

profile of v1, /device:TPU:1, one launch (start us, length us, event | category | flops | bytes accessed | tf_op | source)
XLA Modules:
  0.0 454.8 jit_solution(6904293059433537144)
XLA Ops:
  0.6 18.9 %fusion.10 = (f32[32,128,1,128]{3,2,1,0:T(1,128)S(1)}, f32[32,128,1,128]{3,2,1,0:T(1,128)S(1)}, f32[32,128,1,128]{3,2,1,0:T(1,128)S(1)}, f32[32,128,1,128]{3,2,1,0:T(1,128)S(1)}) fusion(f32[32,128,4,128]{3,2,1,0:T(4,128)} %param.3), kind=kLoop, calls=%fused_computation.45 | loop fusion | bytes 16777216 | tf_op jit(solution)/shard_map/slice | solution.py:126
  20.7 2.1 collective-permute-start
  22.8 2.3 fusion.11
  25.9 3.3 collective-permute-start.1
  31.1 2.1 collective-permute-start.5
  33.2 2.4 copy_bitcast_fusion
  35.7 1.9 collective-permute-start.3
  37.6 18.8 %fusion.9 = (f32[32,128,1,128]{3,2,1,0:T(1,128)S(1)}, f32[32,128,1,128]{3,2,1,0:T(1,128)S(1)}, f32[32,128,1,128]{3,2,1,0:T(1,128)S(1)}, f32[32,128,1,128]{3,2,1,0:T(1,128)S(1)}) fusion(f32[32,128,4,128]{3,2,1,0:T(4,128)} %param.4), kind=kLoop, calls=%fused_computation.44 | loop fusion | bytes 16777216 | tf_op jit(solution)/shard_map/slice | solution.py:129
  57.0 2.1 collective-permute-start.4
  59.2 18.9 %fusion.8 = (f32[32,128,1,128]{3,2,1,0:T(1,128)S(1)}, f32[32,128,1,128]{3,2,1,0:T(1,128)S(1)}, f32[32,128,1,128]{3,2,1,0:T(1,128)S(1)}, f32[32,128,1,128]{3,2,1,0:T(1,128)S(1)}) fusion(f32[32,128,4,128]{3,2,1,0:T(4,128)} %param.5), kind=kLoop, calls=%fused_computation.43 | loop fusion | bytes 16777216 | tf_op jit(solution)/shard_map/slice | solution.py:130
  83.1 2.3 collective-permute-start.11
  85.4 34.4 %collective-permute-done.5 = f32[32,128,128]{2,0,1:T(8,128)} collective-permute-done((f32[32,128,128]{2,0,1:T(8,128)S(1)}, f32[32,128,128]{2,0,1:T(8,128)}, u32[]{:S(2)}, u32[]{:S(2)}) %collective-permute-start.5) | collective-permute-done | bytes 2097184 | tf_op jit(solution)/shard_map/ppermute | solution.py:14
  119.8 2.8 copy.30.refs_4_
  125.2 5.3 %collective-permute-start.12 = (f32[3,128,128]{2,1,0:T(8,128)S(1)}, f32[3,128,128]{2,1,0:T(8,128)S(1)}, u32[]{:S(2)}, u32[]{:S(2)}) collective-permute-start(f32[3,128,128]{2,1,0:T(8,128)S(1)} %pad_maximum_fusion.2), channel_id=1, source_target_pairs={{0,32},{32,64},{64,96},{96,0},{1,33},{33,65},{65,97},{97,1},{2,34}... | collective-permute-start | bytes 589832 | tf_op jit(solution)/shard_map/ppermute | solution.py:14
  130.7 1.7 collective-permute-start.14
  132.4 3.6 collective-permute-done.14.refs_9_
  136.0 1.8 collective-permute-start.15
  139.2 5.0 %collective-permute-start.7 = (f32[1,128,128]{2,1,0:T(8,128)S(1)}, f32[1,128,128]{2,1,0:T(8,128)S(1)}, u32[]{:S(2)}, u32[]{:S(2)}) collective-permute-start(f32[1,128,128]{2,1,0:T(8,128)S(1)} %get-tuple-element.109), channel_id=1, source_target_pairs={{0,32},{32,64},{64,96},{96,0},{1,33},{33,65},{65,97},{97,1},{2,34}... | collective-permute-start | bytes 196616 | tf_op jit(solution)/shard_map/ppermute | solution.py:14
  144.2 67.6 %collective-permute-done.12.refs_7_ = f32[3,128,128]{2,1,0:T(8,128)S(1)} collective-permute-done((f32[3,128,128]{2,1,0:T(8,128)S(1)}, f32[3,128,128]{2,1,0:T(8,128)S(1)}, u32[]{:S(2)}, u32[]{:S(2)}) %collective-permute-start.12) | collective-permute-done | bytes 196640 | tf_op jit(solution)/shard_map/ppermute | solution.py:14
  211.8 3.6 collective-permute-start.8
  216.5 1.8 collective-permute-start.9
  223.1 2.3 collective-permute-start.10
  227.4 2.7 collective-permute-start.21
  231.7 1.8 collective-permute-start.19
  233.5 3.2 collective-permute-done.19.refs_9_
  236.7 1.5 collective-permute-start.20
  238.2 1.7 collective-permute-done.20.refs_10_
  239.9 4.7 %collective-permute-start.22 = (f32[1,128,128]{2,1,0:T(8,128)S(1)}, f32[1,128,128]{2,1,0:T(8,128)S(1)}, u32[]{:S(2)}, u32[]{:S(2)}) collective-permute-start(f32[1,128,128]{2,1,0:T(8,128)S(1)} %get-tuple-element.81), channel_id=1, source_target_pairs={{0,32},{32,64},{64,96},{96,0},{1,33},{33,65},{65,97},{97,1},{2,34}... | collective-permute-start | bytes 196616 | tf_op jit(solution)/shard_map/ppermute | solution.py:14
  244.6 72.6 %collective-permute-done.17.refs_7_ = f32[3,128,128]{2,1,0:T(8,128)S(1)} collective-permute-done((f32[3,128,128]{2,1,0:T(8,128)S(1)}, f32[3,128,128]{2,1,0:T(8,128)S(1)}, u32[]{:S(2)}, u32[]{:S(2)}) %collective-permute-start.17) | collective-permute-done | bytes 196640 | tf_op jit(solution)/shard_map/ppermute | solution.py:14
  317.2 2.8 collective-permute-start.23
  320.0 1.7 collective-permute-start.24
  327.6 1.9 collective-permute-done.25.refs_10_
  331.3 4.4 collective-permute-start.31
  337.3 2.8 collective-permute-done.33.refs_9_
  341.4 1.9 collective-permute-done.34.refs_10_
  343.3 5.2 %collective-permute-start.27 = (f32[1,128,128]{2,1,0:T(8,128)S(1)}, f32[1,128,128]{2,1,0:T(8,128)S(1)}, u32[]{:S(2)}, u32[]{:S(2)}) collective-permute-start(f32[1,128,128]{2,1,0:T(8,128)S(1)} %get-tuple-element.77), channel_id=1, source_target_pairs={{0,32},{32,64},{64,96},{96,0},{1,33},{33,65},{65,97},{97,1},{2,34}... | collective-permute-start | bytes 196616 | tf_op jit(solution)/shard_map/ppermute | solution.py:14
  348.5 71.8 %collective-permute-done.31.refs_7_ = f32[3,128,128]{2,1,0:T(8,128)S(1)} collective-permute-done((f32[3,128,128]{2,1,0:T(8,128)S(1)}, f32[3,128,128]{2,1,0:T(8,128)S(1)}, u32[]{:S(2)}, u32[]{:S(2)}) %collective-permute-start.31) | collective-permute-done | bytes 196640 | tf_op jit(solution)/shard_map/ppermute | solution.py:14
  420.4 4.6 %collective-permute-start.28 = (f32[1,128,128]{2,1,0:T(8,128)S(1)}, f32[1,128,128]{2,1,0:T(8,128)S(1)}, u32[]{:S(2)}, u32[]{:S(2)}) collective-permute-start(f32[1,128,128]{2,1,0:T(8,128)S(1)} %get-tuple-element.76), channel_id=1, source_target_pairs={{0,96},{32,0},{64,32},{96,64},{1,97},{33,1},{65,33},{97,65},{2,98}... | collective-permute-start | bytes 196616 | tf_op jit(solution)/shard_map/ppermute | solution.py:14
  427.3 1.5 update.29
  428.8 1.7 update.31
  430.6 1.7 collective-permute-start.30
  432.2 1.7 update.30
  434.2 2.5 collective-permute-start.40
  436.8 1.5 update.27
  439.0 2.0 collective-permute-start.37
  441.0 2.6 collective-permute-done.36.refs_5_
  444.1 3.8 collective-permute-done.38.refs_7_
  447.9 6.4 %finish.1 = (f32[32,512,128]{2,1,0:T(8,128)}, f32[32,512,128]{2,1,0:T(8,128)}) custom-call(f32[32,128,128]{2,1,0:T(8,128)S(1)} %get-tuple-element.16.refs_0_, f32[32,128,128]{2,1,0:T(8,128)S(1)} %get-tuple-element.17.refs_1_, f32[32,128,128]{2,1,0:T(8,128)S(1)} %get-tuple-element.32.refs_2_, f32[32,128,128]{2,1,0:T(8,128)S(1)} %get-tuple-element.38.refs_3_, ...), custom_call_target="tpu_custom_call" | custom-call | flops 41943040 | bytes 25165824 | tf_op jit(solution)/shard_map/finish/pallas_call | solution.py:107
  (111 shorter events, 37.2 us)
Async XLA Ops:
  20.7 59.9 %collective-permute-start = (f32[32,128,128]{2,0,1:T(8,128)S(1)}, f32[32,128,128]{2,0,1:T(8,128)S(1)}, u32[]{:S(2)}, u32[]{:S(2)}) collective-permute-start(f32[32,128,128]{2,0,1:T(8,128)S(1)} %bitcast.226), channel_id=1, source_target_pairs={{0,1},{1,2},{2,3},{3,4},{4,5},{5,6},{6,7},{7,0},{8,9},{9,10},{10,1... | collective-permute-start | bytes 6291464 | tf_op jit(solution)/shard_map/ppermute | solution.py:14
  25.9 52.2 %collective-permute-start.1 = (f32[4,128,128]{2,1,0:T(8,128)}, f32[4,128,128]{2,1,0:T(8,128)S(1)}, u32[]{:S(2)}, u32[]{:S(2)}) collective-permute-start(f32[4,128,128]{2,1,0:T(8,128)} %pad_maximum_fusion), channel_id=1, source_target_pairs={{0,32},{32,64},{64,96},{96,0},{1,33},{33,65},{65,97},{97,1},{2,34}... | collective-permute-start | bytes 786440 | tf_op jit(solution)/shard_map/ppermute | solution.py:14
  29.9 48.2 %collective-permute-start.2 = (f32[4,128,128]{2,1,0:T(8,128)}, f32[4,128,128]{2,1,0:T(8,128)S(1)}, u32[]{:S(2)}, u32[]{:S(2)}) collective-permute-start(f32[4,128,128]{2,1,0:T(8,128)} %pad_maximum_fusion.1), channel_id=1, source_target_pairs={{0,96},{32,0},{64,32},{96,64},{1,97},{33,1},{65,33},{97,65},{2,98}... | collective-permute-start | bytes 786440 | tf_op jit(solution)/shard_map/ppermute | solution.py:14
  31.1 88.7 %collective-permute-start.5 = (f32[32,128,128]{2,0,1:T(8,128)S(1)}, f32[32,128,128]{2,0,1:T(8,128)}, u32[]{:S(2)}, u32[]{:S(2)}) collective-permute-start(f32[32,128,128]{2,0,1:T(8,128)S(1)} %bitcast.228), channel_id=1, source_target_pairs={{0,7},{1,0},{2,1},{3,2},{4,3},{5,4},{6,5},{7,6},{8,15},{9,8},{10,9... | collective-permute-start | bytes 6291464 | tf_op jit(solution)/shard_map/ppermute | solution.py:14
  35.7 21.3 %collective-permute-start.3 = (f32[4,32,128]{2,1,0:T(8,128)S(1)}, f32[4,32,128]{2,1,0:T(8,128)S(1)}, u32[]{:S(2)}, u32[]{:S(2)}) collective-permute-start(f32[4,32,128]{2,1,0:T(8,128)S(1)} %pad_maximum_fusion.8), channel_id=1, source_target_pairs={{0,8},{8,16},{16,24},{24,0},{1,9},{9,17},{17,25},{25,1},{2,10},{10... | collective-permute-start | bytes 196616 | tf_op jit(solution)/shard_map/ppermute | solution.py:14
  57.0 21.1 %collective-permute-start.4 = (f32[4,32,128]{2,1,0:T(8,128)}, f32[4,32,128]{2,1,0:T(8,128)S(1)}, u32[]{:S(2)}, u32[]{:S(2)}) collective-permute-start(f32[4,32,128]{2,1,0:T(8,128)} %pad_maximum_fusion.9), channel_id=1, source_target_pairs={{0,24},{8,0},{16,8},{24,16},{1,25},{9,1},{17,9},{25,17},{2,26},{10... | collective-permute-start | bytes 196616 | tf_op jit(solution)/shard_map/ppermute | solution.py:14
  83.1 137.7 %collective-permute-start.11 = (f32[32,128,128]{2,1,0:T(8,128)S(1)}, f32[32,128,128]{2,1,0:T(8,128)S(1)}, u32[]{:S(2)}, u32[]{:S(2)}) collective-permute-start(f32[32,128,128]{2,1,0:T(8,128)S(1)} %update.16.refs_0_.refs_1_.refs_2_.refs_3_), channel_id=1, source_target_pairs={{0,7},{1,0},{2,1},{3,2},{4,3},{5,4},{6,5},{7,6},{8,15},{9,8},{10,9... | collective-permute-start | bytes 6291464 | tf_op jit(solution)/shard_map/ppermute | solution.py:14
  123.9 102.3 %collective-permute-start.6 = (f32[32,128,128]{2,1,0:T(8,128)S(1)}, f32[32,128,128]{2,1,0:T(8,128)S(1)}, u32[]{:S(2)}, u32[]{:S(2)}) collective-permute-start(f32[32,128,128]{2,1,0:T(8,128)S(1)} %update.17.refs_0_.refs_1_.refs_2_.refs_4_), channel_id=1, source_target_pairs={{0,1},{1,2},{2,3},{3,4},{4,5},{5,6},{6,7},{7,0},{8,9},{9,10},{10,1... | collective-permute-start | bytes 6291464 | tf_op jit(solution)/shard_map/ppermute | solution.py:14
  125.2 86.6 %collective-permute-start.12 = (f32[3,128,128]{2,1,0:T(8,128)S(1)}, f32[3,128,128]{2,1,0:T(8,128)S(1)}, u32[]{:S(2)}, u32[]{:S(2)}) collective-permute-start(f32[3,128,128]{2,1,0:T(8,128)S(1)} %pad_maximum_fusion.2), channel_id=1, source_target_pairs={{0,32},{32,64},{64,96},{96,0},{1,33},{33,65},{65,97},{97,1},{2,34}... | collective-permute-start | bytes 589832 | tf_op jit(solution)/shard_map/ppermute | solution.py:14
  130.6 86.0 %collective-permute-start.13 = (f32[3,128,128]{2,1,0:T(8,128)S(1)}, f32[3,128,128]{2,1,0:T(8,128)S(1)}, u32[]{:S(2)}, u32[]{:S(2)}) collective-permute-start(f32[3,128,128]{2,1,0:T(8,128)S(1)} %pad_maximum_fusion.3), channel_id=1, source_target_pairs={{0,96},{32,0},{64,32},{96,64},{1,97},{33,1},{65,33},{97,65},{2,98}... | collective-permute-start | bytes 589832 | tf_op jit(solution)/shard_map/ppermute | solution.py:14
  130.7 5.3 %collective-permute-start.14 = (f32[3,32,128]{2,1,0:T(8,128)S(1)}, f32[3,32,128]{2,1,0:T(8,128)S(1)}, u32[]{:S(2)}, u32[]{:S(2)}) collective-permute-start(f32[3,32,128]{2,1,0:T(8,128)S(1)} %pad_maximum_fusion.10), channel_id=1, source_target_pairs={{0,8},{8,16},{16,24},{24,0},{1,9},{9,17},{17,25},{25,1},{2,10},{10... | collective-permute-start | bytes 147464 | tf_op jit(solution)/shard_map/ppermute | solution.py:14
  136.0 3.2 collective-permute-start.15
  139.2 87.0 %collective-permute-start.7 = (f32[1,128,128]{2,1,0:T(8,128)S(1)}, f32[1,128,128]{2,1,0:T(8,128)S(1)}, u32[]{:S(2)}, u32[]{:S(2)}) collective-permute-start(f32[1,128,128]{2,1,0:T(8,128)S(1)} %get-tuple-element.109), channel_id=1, source_target_pairs={{0,32},{32,64},{64,96},{96,0},{1,33},{33,65},{65,97},{97,1},{2,34}... | collective-permute-start | bytes 196616 | tf_op jit(solution)/shard_map/ppermute | solution.py:14
  211.8 14.4 %collective-permute-start.8 = (f32[1,128,128]{2,1,0:T(8,128)S(1)}, f32[1,128,128]{2,1,0:T(8,128)S(1)}, u32[]{:S(2)}, u32[]{:S(2)}) collective-permute-start(f32[1,128,128]{2,1,0:T(8,128)S(1)} %get-tuple-element.108), channel_id=1, source_target_pairs={{0,96},{32,0},{64,32},{96,64},{1,97},{33,1},{65,33},{97,65},{2,98}... | collective-permute-start | bytes 196616 | tf_op jit(solution)/shard_map/ppermute | solution.py:14
  216.5 6.5 %collective-permute-start.9 = (f32[1,32,128]{2,1,0:T(8,128)S(1)}, f32[1,32,128]{2,1,0:T(8,128)S(1)}, u32[]{:S(2)}, u32[]{:S(2)}) collective-permute-start(f32[1,32,128]{2,1,0:T(8,128)S(1)} %bitcast.260), channel_id=1, source_target_pairs={{0,8},{8,16},{16,24},{24,0},{1,9},{9,17},{17,25},{25,1},{2,10},{10... | collective-permute-start | bytes 49160 | tf_op jit(solution)/shard_map/ppermute | solution.py:14
  222.0 102.2 %collective-permute-start.16 = (f32[32,128,128]{2,1,0:T(8,128)S(1)}, f32[32,128,128]{2,1,0:T(8,128)S(1)}, u32[]{:S(2)}, u32[]{:S(2)}) collective-permute-start(f32[32,128,128]{2,1,0:T(8,128)S(1)} %update.21.refs_0_.refs_1_.refs_2_.refs_4_), channel_id=1, source_target_pairs={{0,1},{1,2},{2,3},{3,4},{4,5},{5,6},{6,7},{7,0},{8,9},{9,10},{10,1... | collective-permute-start | bytes 6291464 | tf_op jit(solution)/shard_map/ppermute | solution.py:14
  223.1 3.1 collective-permute-start.10
  227.4 102.1 %collective-permute-start.21 = (f32[32,128,128]{2,1,0:T(8,128)S(1)}, f32[32,128,128]{2,1,0:T(8,128)S(1)}, u32[]{:S(2)}, u32[]{:S(2)}) collective-permute-start(f32[32,128,128]{2,1,0:T(8,128)S(1)} %update.19.refs_0_.refs_1_.refs_2_.refs_3_), channel_id=1, source_target_pairs={{0,7},{1,0},{2,1},{3,2},{4,3},{5,4},{6,5},{7,6},{8,15},{9,8},{10,9... | collective-permute-start | bytes 6291464 | tf_op jit(solution)/shard_map/ppermute | solution.py:14
  230.2 87.0 %collective-permute-start.17 = (f32[3,128,128]{2,1,0:T(8,128)S(1)}, f32[3,128,128]{2,1,0:T(8,128)S(1)}, u32[]{:S(2)}, u32[]{:S(2)}) collective-permute-start(f32[3,128,128]{2,1,0:T(8,128)S(1)} %pad_maximum_fusion.4), channel_id=1, source_target_pairs={{0,32},{32,64},{64,96},{96,0},{1,33},{33,65},{65,97},{97,1},{2,34}... | collective-permute-start | bytes 589832 | tf_op jit(solution)/shard_map/ppermute | solution.py:14
  231.6 88.4 %collective-permute-start.18 = (f32[3,128,128]{2,1,0:T(8,128)S(1)}, f32[3,128,128]{2,1,0:T(8,128)S(1)}, u32[]{:S(2)}, u32[]{:S(2)}) collective-permute-start(f32[3,128,128]{2,1,0:T(8,128)S(1)} %pad_maximum_fusion.5), channel_id=1, source_target_pairs={{0,96},{32,0},{64,32},{96,64},{1,97},{33,1},{65,33},{97,65},{2,98}... | collective-permute-start | bytes 589832 | tf_op jit(solution)/shard_map/ppermute | solution.py:14
  231.7 5.0 %collective-permute-start.19 = (f32[3,32,128]{2,1,0:T(8,128)S(1)}, f32[3,32,128]{2,1,0:T(8,128)S(1)}, u32[]{:S(2)}, u32[]{:S(2)}) collective-permute-start(f32[3,32,128]{2,1,0:T(8,128)S(1)} %pad_maximum_fusion.12), channel_id=1, source_target_pairs={{0,8},{8,16},{16,24},{24,0},{1,9},{9,17},{17,25},{25,1},{2,10},{10... | collective-permute-start | bytes 147464 | tf_op jit(solution)/shard_map/ppermute | solution.py:14
  236.7 3.2 collective-permute-start.20
  239.9 89.6 %collective-permute-start.22 = (f32[1,128,128]{2,1,0:T(8,128)S(1)}, f32[1,128,128]{2,1,0:T(8,128)S(1)}, u32[]{:S(2)}, u32[]{:S(2)}) collective-permute-start(f32[1,128,128]{2,1,0:T(8,128)S(1)} %get-tuple-element.81), channel_id=1, source_target_pairs={{0,32},{32,64},{64,96},{96,0},{1,33},{33,65},{65,97},{97,1},{2,34}... | collective-permute-start | bytes 196616 | tf_op jit(solution)/shard_map/ppermute | solution.py:14
  317.2 12.3 %collective-permute-start.23 = (f32[1,128,128]{2,1,0:T(8,128)S(1)}, f32[1,128,128]{2,1,0:T(8,128)S(1)}, u32[]{:S(2)}, u32[]{:S(2)}) collective-permute-start(f32[1,128,128]{2,1,0:T(8,128)S(1)} %get-tuple-element.80), channel_id=1, source_target_pairs={{0,96},{32,0},{64,32},{96,64},{1,97},{33,1},{65,33},{97,65},{2,98}... | collective-permute-start | bytes 196616 | tf_op jit(solution)/shard_map/ppermute | solution.py:14
  320.0 6.5 %collective-permute-start.24 = (f32[1,32,128]{2,1,0:T(8,128)S(1)}, f32[1,32,128]{2,1,0:T(8,128)S(1)}, u32[]{:S(2)}, u32[]{:S(2)}) collective-permute-start(f32[1,32,128]{2,1,0:T(8,128)S(1)} %bitcast.261), channel_id=1, source_target_pairs={{0,8},{8,16},{16,24},{24,0},{1,9},{9,17},{17,25},{25,1},{2,10},{10... | collective-permute-start | bytes 49160 | tf_op jit(solution)/shard_map/ppermute | solution.py:14
  325.4 105.2 %collective-permute-start.35 = (f32[32,128,128]{2,1,0:T(8,128)S(1)}, f32[32,128,128]{2,1,0:T(8,128)S(1)}, u32[]{:S(2)}, u32[]{:S(2)}) collective-permute-start(f32[32,128,128]{2,1,0:T(8,128)S(1)} %update.24.refs_0_.refs_1_.refs_2_.refs_3_), channel_id=1, source_target_pairs={{0,7},{1,0},{2,1},{3,2},{4,3},{5,4},{6,5},{7,6},{8,15},{9,8},{10,9... | collective-permute-start | bytes 6291464 | tf_op jit(solution)/shard_map/ppermute | solution.py:14
  326.6 3.0 collective-permute-start.25
  330.8 106.0 %collective-permute-start.26 = (f32[32,128,128]{2,1,0:T(8,128)S(1)}, f32[32,128,128]{2,1,0:T(8,128)S(1)}, u32[]{:S(2)}, u32[]{:S(2)}) collective-permute-start(f32[32,128,128]{2,1,0:T(8,128)S(1)} %update.25), channel_id=1, source_target_pairs={{0,1},{1,2},{2,3},{3,4},{4,5},{5,6},{6,7},{7,0},{8,9},{9,10},{10,1... | collective-permute-start | bytes 6291464 | tf_op jit(solution)/shard_map/ppermute | solution.py:14
  331.3 89.1 %collective-permute-start.31 = (f32[3,128,128]{2,1,0:T(8,128)S(1)}, f32[3,128,128]{2,1,0:T(8,128)S(1)}, u32[]{:S(2)}, u32[]{:S(2)}) collective-permute-start(f32[3,128,128]{2,1,0:T(8,128)S(1)} %pad_maximum_fusion.6), channel_id=1, source_target_pairs={{0,32},{32,64},{64,96},{96,0},{1,33},{33,65},{65,97},{97,1},{2,34}... | collective-permute-start | bytes 589832 | tf_op jit(solution)/shard_map/ppermute | solution.py:14
  335.7 90.2 %collective-permute-start.32 = (f32[3,128,128]{2,1,0:T(8,128)S(1)}, f32[3,128,128]{2,1,0:T(8,128)S(1)}, u32[]{:S(2)}, u32[]{:S(2)}) collective-permute-start(f32[3,128,128]{2,1,0:T(8,128)S(1)} %pad_maximum_fusion.7), channel_id=1, source_target_pairs={{0,96},{32,0},{64,32},{96,64},{1,97},{33,1},{65,33},{97,65},{2,98}... | collective-permute-start | bytes 589832 | tf_op jit(solution)/shard_map/ppermute | solution.py:14
  335.8 4.2 collective-permute-start.33
  340.1 3.2 collective-permute-start.34
  343.3 93.5 %collective-permute-start.27 = (f32[1,128,128]{2,1,0:T(8,128)S(1)}, f32[1,128,128]{2,1,0:T(8,128)S(1)}, u32[]{:S(2)}, u32[]{:S(2)}) collective-permute-start(f32[1,128,128]{2,1,0:T(8,128)S(1)} %get-tuple-element.77), channel_id=1, source_target_pairs={{0,32},{32,64},{64,96},{96,0},{1,33},{33,65},{65,97},{97,1},{2,34}... | collective-permute-start | bytes 196616 | tf_op jit(solution)/shard_map/ppermute | solution.py:14
  420.4 16.4 %collective-permute-start.28 = (f32[1,128,128]{2,1,0:T(8,128)S(1)}, f32[1,128,128]{2,1,0:T(8,128)S(1)}, u32[]{:S(2)}, u32[]{:S(2)}) collective-permute-start(f32[1,128,128]{2,1,0:T(8,128)S(1)} %get-tuple-element.76), channel_id=1, source_target_pairs={{0,96},{32,0},{64,32},{96,64},{1,97},{33,1},{65,33},{97,65},{2,98}... | collective-permute-start | bytes 196616 | tf_op jit(solution)/shard_map/ppermute | solution.py:14
  425.9 8.1 %collective-permute-start.29 = (f32[1,32,128]{2,1,0:T(8,128)S(1)}, f32[1,32,128]{2,1,0:T(8,128)S(1)}, u32[]{:S(2)}, u32[]{:S(2)}) collective-permute-start(f32[1,32,128]{2,1,0:T(8,128)S(1)} %bitcast.257), channel_id=1, source_target_pairs={{0,8},{8,16},{16,24},{24,0},{1,9},{9,17},{17,25},{25,1},{2,10},{10... | collective-permute-start | bytes 49160 | tf_op jit(solution)/shard_map/ppermute | solution.py:14
  430.6 3.6 collective-permute-start.30
  434.0 13.9 %collective-permute-start.39 = (f32[6,32,128]{2,1,0:T(8,128)S(1)}, f32[6,32,128]{2,1,0:T(8,128)S(1)}, u32[]{:S(2)}, u32[]{:S(2)}) collective-permute-start(f32[6,32,128]{2,1,0:T(8,128)S(1)} %bitcast_dynamic-update-slice_fusion.refs_8_), channel_id=1, source_target_pairs={{0,8},{8,16},{16,24},{24,0},{1,9},{9,17},{17,25},{25,1},{2,10},{10... | collective-permute-start | bytes 294920 | tf_op jit(solution)/shard_map/ppermute | solution.py:14
  434.2 13.7 %collective-permute-start.40 = (f32[6,32,128]{2,1,0:T(8,128)S(1)}, f32[6,32,128]{2,1,0:T(8,128)S(1)}, u32[]{:S(2)}, u32[]{:S(2)}) collective-permute-start(f32[6,32,128]{2,1,0:T(8,128)S(1)} %bitcast_dynamic-update-slice_fusion.refs_8_), channel_id=1, source_target_pairs={{0,24},{8,0},{16,8},{24,16},{1,25},{9,1},{17,9},{25,17},{2,26},{10... | collective-permute-start | bytes 294920 | tf_op jit(solution)/shard_map/ppermute | solution.py:14
  436.8 11.1 %collective-permute-start.41 = (f32[6,32,128]{2,1,0:T(8,128)S(1)}, f32[6,32,128]{2,1,0:T(8,128)S(1)}, u32[]{:S(2)}, u32[]{:S(2)}) collective-permute-start(f32[6,32,128]{2,1,0:T(8,128)S(1)} %bitcast_dynamic-update-slice_fusion.refs_8_), channel_id=1, source_target_pairs={{0,16},{8,24},{16,0},{24,8},{1,17},{9,25},{17,1},{25,9},{2,18},{10... | collective-permute-start | bytes 294920 | tf_op jit(solution)/shard_map/ppermute | solution.py:14
  438.3 5.4 %collective-permute-start.36 = (f32[2,32,128]{2,1,0:T(8,128)S(1)}, f32[2,32,128]{2,1,0:T(8,128)S(1)}, u32[]{:S(2)}, u32[]{:S(2)}) collective-permute-start(f32[2,32,128]{2,1,0:T(8,128)S(1)} %pad_maximum_fusion.16.refs_4_), channel_id=1, source_target_pairs={{0,8},{8,16},{16,24},{24,0},{1,9},{9,17},{17,25},{25,1},{2,10},{10... | collective-permute-start | bytes 98312 | tf_op jit(solution)/shard_map/ppermute | solution.py:14
  439.0 5.1 %collective-permute-start.37 = (f32[2,32,128]{2,1,0:T(8,128)S(1)}, f32[2,32,128]{2,1,0:T(8,128)S(1)}, u32[]{:S(2)}, u32[]{:S(2)}) collective-permute-start(f32[2,32,128]{2,1,0:T(8,128)S(1)} %pad_maximum_fusion.16.refs_4_), channel_id=1, source_target_pairs={{0,24},{8,0},{16,8},{24,16},{1,25},{9,1},{17,9},{25,17},{2,26},{10... | collective-permute-start | bytes 98312 | tf_op jit(solution)/shard_map/ppermute | solution.py:14
  443.6 4.3 collective-permute-start.38

commit v2 on v1

v2 whole, which is shorter than its diff:
```python
import jax
import jax.numpy as jnp
from jax import lax
from jax.experimental import pallas as pl
from jax.experimental.pallas import tpu as pltpu
from jax.sharding import PartitionSpec as P


STEPS = 4
ROWS = 8


def shift(x, axis, by):
    size = lax.axis_size(axis)
    return lax.ppermute(x, axis, [(i, (i + by) % size) for i in range(size)])


def take_body(parts, whole, *refs):
    outs, sems = refs[:-1], refs[-1]
    copies = []
    for n, (out, part) in enumerate(zip(outs, parts)):
        copies += [
            pltpu.make_async_copy(source(whole), target(out), sems.at[n, k])
            for k, (source, target) in enumerate(part)
        ]
    for copy in copies:
        copy.start()
    for copy in copies:
        copy.wait()


def take(whole, shapes, parts):
    lanes = whole.shape[-1]
    got = pl.pallas_call(
        lambda *refs: take_body(parts, *refs),
        in_specs=[pl.BlockSpec(memory_space=pltpu.HBM)],
        out_specs=[pl.BlockSpec(memory_space=pltpu.VMEM)] * len(shapes),
        out_shape=[jax.ShapeDtypeStruct((*s, 1, lanes), whole.dtype) for s in shapes],
        scratch_shapes=[pltpu.SemaphoreType.DMA((len(parts), max(len(p) for p in parts)))],
        compiler_params=pltpu.CompilerParams(vmem_limit_bytes=2**20),
        cost_estimate=pl.CostEstimate(flops=20_000_000, bytes_accessed=2**22, transcendentals=0),
        name="take",
    )(whole)
    return [g.reshape(*s, lanes) for g, s in zip(got, shapes)]


def plane_of(z, depth, pieces):
    size = depth // pieces

    def piece(k):
        rows = pl.ds(k * size, size)
        return (lambda w: w.at[rows, :, z], lambda o: o.at[rows])

    return [piece(k) for k in range(pieces)]


def edge_of(pick):
    return [(lambda w, z=z: pick(w, z), lambda o, z=z: o.at[z]) for z in range(4)]


def grow_body(plan, last, *refs):
    zs, n_in, base = plan["zs"], plan["n_in"], plan["base"]
    ins, outs = refs[:n_in], refs[n_in:]
    i = pl.program_id(0)
    n = pl.num_programs(0)
    width = ins[0].shape[1]
    place = lax.broadcasted_iota(jnp.int32, ins[0].shape[1:], 0)
    for j, z in enumerate(zs):
        c, low, high, before, after, d, f, south, north, west, east = (ins[a] for a in plan[z])
        rest = outs[len(zs) :]

        @pl.loop(0, ROWS)
        def _(r, c=c, low=low, high=high, before=before, after=after, d=d, f=f, south=south, north=north, west=west, east=east, j=j):
            x = c[r]
            edge_low = jnp.where(i == 0, south[0], before[0])
            edge_high = jnp.where(i == n - 1, north[0], after[0])
            lat_low = jnp.where(r == 0, edge_low, c[jnp.maximum(r - 1, 0)])
            lat_high = jnp.where(r == ROWS - 1, edge_high, c[jnp.minimum(r + 1, ROWS - 1)])
            left = jnp.where(place == 0, west[0, pl.ds(r, 1), :], pltpu.roll(x, 1, 0))
            right = jnp.where(place == width - 1, east[0, pl.ds(r, 1), :], pltpu.roll(x, width - 1, 0))
            spread = lat_low + lat_high + left + right + low[r] + high[r] - 6.0 * x
            y = x + d[r] * spread + f[r]
            outs[j][r] = y
            if last:
                total = jnp.sum(y, axis=0, keepdims=True)
                away = y - total * (1.0 / width)
                rest[0][2 * j, pl.ds(r, 1), :] = total
                rest[0][2 * j + 1, pl.ds(r, 1), :] = jnp.sum(away * away, axis=0, keepdims=True)
            else:
                rest[2][base + j, pl.ds(r, 1), :] = y[width - 1 :, :]
                rest[3][base + j, pl.ds(r, 1), :] = y[:1, :]

        if not last:

            @pl.when(i == 0)
            def _(j=j):
                rest[1][base + j] = outs[j][0]

            @pl.when(i == n - 1)
            def _(j=j):
                rest[0][base + j] = outs[j][ROWS - 1]

    if plan["carried"]:
        held = [ins[a] for a in plan["carried"]]
        rest[2][:base] = held[2][...]
        rest[3][:base] = held[3][...]

        @pl.when(i == 0)
        def _():
            rest[0][:base] = held[0][...]
            rest[1][:base] = held[1][...]


def grow(zs, u, low, high, d, f, where, last, carried=()):
    depth, width, lanes = u[0].shape
    block = pl.BlockSpec((ROWS, width, lanes), lambda i: (i, 0, 0))
    row_before = pl.BlockSpec((1, width, lanes), lambda i: (jnp.maximum(i * ROWS - 1, 0), 0, 0))
    row_after = pl.BlockSpec((1, width, lanes), lambda i: (jnp.minimum(i * ROWS + ROWS, depth - 1), 0, 0))
    arrays, specs, seen = [], [], {}

    def use(key, array, spec):
        if key not in seen:
            seen[key] = len(arrays)
            arrays.append(array)
            specs.append(spec)
        return seen[key]

    plan = {"zs": zs}
    for z in zs:
        sides, k = where[z]
        lat_edge = pl.BlockSpec((1, width, lanes), lambda i, k=k: (k, 0, 0))
        lon_edge = pl.BlockSpec((1, ROWS, lanes), lambda i, k=k: (k, i, 0))
        plan[z] = [
            use(("u", z), u[z], block),
            use("low", low, block) if z == 0 else use(("u", z - 1), u[z - 1], block),
            use("high", high, block) if z == 3 else use(("u", z + 1), u[z + 1], block),
            use(("before", z), u[z], row_before),
            use(("after", z), u[z], row_after),
            use(("d", z), d[z], block),
            use(("f", z), f[z], block),
            use(("s", z), sides[0], lat_edge),
            use(("n", z), sides[1], lat_edge),
            use(("w", z), sides[2], lon_edge),
            use(("e", z), sides[3], lon_edge),
        ]
    m = len(zs)
    base = carried[0].shape[0] if carried else 0
    lat_all = pl.BlockSpec((base, width, lanes), lambda i: (0, 0, 0))
    lon_all = pl.BlockSpec((base, ROWS, lanes), lambda i: (0, i, 0))
    plan["carried"] = [
        use(("carried", k), a, spec) for k, (a, spec) in enumerate(zip(carried, (lat_all, lat_all, lon_all, lon_all)))
    ]
    plan["base"], plan["n_in"] = base, len(arrays)
    shapes, outs = [u[0].shape] * m, [block] * m
    if last:
        shapes += [(2 * m, depth, lanes)]
        outs += [pl.BlockSpec((2 * m, ROWS, lanes), lambda i: (0, i, 0))]
    else:
        t = base + m
        shapes += [(t, width, lanes)] * 2 + [(t, depth, lanes)] * 2
        outs += [pl.BlockSpec((t, width, lanes), lambda i: (0, 0, 0))] * 2
        outs += [pl.BlockSpec((t, ROWS, lanes), lambda i: (0, i, 0))] * 2
    got = pl.pallas_call(
        lambda *refs: grow_body(plan, last, *refs),
        grid=(depth // ROWS,),
        in_specs=specs,
        out_specs=outs,
        out_shape=[jax.ShapeDtypeStruct(s, u[0].dtype) for s in shapes],
        compiler_params=pltpu.CompilerParams(vmem_limit_bytes=(8 if m == 1 else 16) * 2**20),
        cost_estimate=pl.CostEstimate(flops=10_000_000 * m, bytes_accessed=2**22 * m, transcendentals=0),
        name="grow",
    )(*arrays)
    return got[:m], got[m:]


def exchange(south, north, east, west):
    return (
        shift(south, "lat", 1),
        shift(north, "lat", -1),
        shift(east, "lon", 1),
        shift(west, "lon", -1),
    )


def finish_body(count, *refs):
    planes, stats, (score, end) = refs[:4], refs[4:-2], refs[-2:]
    width = planes[0].shape[1]
    for z in range(4):
        group, k = (0, 0) if z == 0 else (1, 3 - z)
        sums = [stats[4 * group + j][2 * k] for j in range(4)]
        powers = [stats[4 * group + j][2 * k + 1] for j in range(4)]
        mean = (sums[0] + sums[1] + sums[2] + sums[3]) * (1.0 / count)
        power = powers[0] + powers[1] + powers[2] + powers[3]
        for s in sums:
            gap = s * (1.0 / width) - mean
            power = power + width * (gap * gap)
        scale = lax.rsqrt(power * (1.0 / count) + 0.0001)
        for r in range(ROWS):
            centre, factor = mean[r : r + 1, :], scale[r : r + 1, :]
            y = planes[z][r]
            end[r, pl.ds(z, width, stride=4), :] = y
            score[r, pl.ds(z, width, stride=4), :] = (y - centre) * factor


def finish(planes, edge_stats, inner_stats):
    depth, width, lanes = planes[0].shape
    block = pl.BlockSpec((ROWS, width, lanes), lambda i: (i, 0, 0))
    wide = pl.BlockSpec((ROWS, 4 * width, lanes), lambda i: (i, 0, 0))
    edge = pl.BlockSpec((2, ROWS, lanes), lambda i: (0, i, 0))
    inner = pl.BlockSpec((6, ROWS, lanes), lambda i: (0, i, 0))
    count = width * lax.axis_size("lon")
    full = jax.ShapeDtypeStruct((depth, 4 * width, lanes), planes[0].dtype)
    score, end = pl.pallas_call(
        lambda *refs: finish_body(count, *refs),
        grid=(depth // ROWS,),
        in_specs=[block] * 4 + [edge] * 4 + [inner] * 4,
        out_specs=[wide] * 2,
        out_shape=[full] * 2,
        compiler_params=pltpu.CompilerParams(vmem_limit_bytes=24 * 2**20),
        cost_estimate=pl.CostEstimate(flops=40_000_000, bytes_accessed=12 * 4 * planes[0].size, transcendentals=0),
        name="finish",
    )(*planes, *edge_stats, *inner_stats)
    shape = (depth, width, 4, lanes)
    return score.reshape(shape), end.reshape(shape)


def from_all(x):
    return [x] + [shift(x, "lon", by) for by in (1, -1, 2)]


def local(initial_heat, diffusivity_ratio, forcing_term):
    depth, width, _, lanes = initial_heat.shape
    plane = (depth, width)
    views = [a.reshape(depth, width, 4, 1, lanes) for a in (initial_heat, diffusivity_ratio, forcing_term)]
    u = [None] * 4
    (u[3],) = take(views[0], [plane], [plane_of(3, depth, 8)])
    up = shift(u[3], "lev", 1)
    u[0], south, north, east, west = take(
        views[0],
        [plane, (4, width), (4, width), (4, depth), (4, depth)],
        [
            plane_of(0, depth, 8),
            edge_of(lambda w, z: w.at[depth - 1, :, z]),
            edge_of(lambda w, z: w.at[0, :, z]),
            edge_of(lambda w, z: w.at[:, width - 1, z]),
            edge_of(lambda w, z: w.at[:, 0, z]),
        ],
    )
    whole = exchange(south, north, east, west)
    down = shift(u[0], "lev", -1)
    u[1], u[2] = take(views[0], [plane] * 2, [plane_of(z, depth, 8) for z in (1, 2)])
    d = take(views[1], [plane] * 4, [plane_of(z, depth, 8) for z in range(4)])
    f = take(views[2], [plane] * 4, [plane_of(z, depth, 8) for z in range(4)])
    where = [(whole, z) for z in range(4)]
    for step in range(STEPS):
        last = step == STEPS - 1
        first, second = (0, 3) if step % 2 == 0 else (3, 0)
        v = [None] * 4
        faces, stats = {}, {}
        carried = ()
        most = (first, 1, 2) if first == 0 else (3, 2, 1)
        for slot, zs in (("a", most), ("b", (second,))):
            made, rest = grow(zs, u, up, down, d, f, where, last, carried)
            for z, plane_made in zip(zs, made):
                v[z] = plane_made
            if last:
                stats[slot] = from_all(rest[0])
                continue
            if slot == "a":
                carried = rest
            else:
                sides = exchange(*rest)
            z = zs[0]
            faces[z] = shift(v[z], "lev", -1 if z == 0 else 1)
        if not last:
            order = most + (second,)
            where = [(sides, order.index(z)) for z in range(4)]
            up, down = faces[3], faces[0]
        u = v
    return finish(u, stats["b"], stats["a"])


def solution(mesh):
    placed = P("lat", "lon", "lev", None)

    return jax.shard_map(
        local,
        mesh=mesh,
        in_specs=(placed,) * 3,
        out_specs=(placed, placed),
        check_vma=False,
    )
```

time: 462 us -> 455 us (0.985); the launches traced: 455 us -> 453 us
  waiting for transfers between devices: 273 us -> 344 us
  local copies, waits for them, and re-layouts: 71.7 us -> 3.39 us
  starting transfers between devices: 82.8 us -> 47.3 us
  Pallas kernels: 24 us -> 57.3 us
    ppermute x42 -> x30, waiting for transfers between devices: 273 us -> 344 us  [shift(): return lax.ppermute(x, axis, [(i, (i + by) % size) for i in range(size)])]
    slice x28 -> x0, local copies, waits for them, and re-layouts: 59.3 us -> none  [the longest x1 18.9 us: local(): f = [forcing_term[:, :, z, :] for z in range(4)]]
    ppermute x42 -> x30, starting transfers between devices: 82.8 us -> 47.3 us  [shift(): return lax.ppermute(x, axis, [(i, (i + by) % size) for i in range(size)])]
    pallas_call x14 -> x13, Pallas kernels: 17.5 us -> 50.8 us  [the longest x8 31.5 us: grow(): pl.pallas_call(lambda *refs: grow_body(plan, last, *refs), grid=(depth //...]
  transfers between devices with their start and end apart: 42 -> 30, of which waited for: 16 -> 17; matrix products, arithmetic and copies ran while one was open for 12% -> 0% of each run, Pallas kernels for 4% -> 11%
where the time goes in v2:
time: 455 us; the launch traced here: 453 us
  waiting for transfers between devices  344 us (76%)
  Pallas kernels  57.3 us (13%)
  starting transfers between devices  47.3 us (10%)
    ppermute x30, waiting for transfers between devices, shift(): return lax.ppermute(x, axis, [(i, (i + by) % size) for i in range(size)])  344 us
    ppermute x30, starting transfers between devices, shift(): return lax.ppermute(x, axis, [(i, (i + by) % size) for i in range(size)])  47.3 us
    pallas_call x8, Pallas kernels, grow(): pl.pallas_call(lambda *refs: grow_body(plan, last, *refs), grid=(depth //...  31.5 us
    pallas_call x5, Pallas kernels, take(): pl.pallas_call(lambda *refs: take_body(parts, *refs), in_specs=[pl.BlockS...  19.3 us
  transfers between devices with their start and end apart: 30, of which 17 were waited for; matrix products, arithmetic and copies ran while one was open for 0% of the time, Pallas kernels for 11%

profile of v2, /device:TPU:1, one launch (start us, length us, event | category | flops | bytes accessed | tf_op | source)
XLA Modules:
  0.0 452.8 jit_solution(14428454373063523735)
XLA Ops:
  0.6 3.4 copy-done
  4.0 1.5 take.6
  5.5 2.1 collective-permute-start
  7.7 2.3 take.5
  10.0 4.3 collective-permute-start.5
  14.3 3.3 collective-permute-start.1
  17.6 1.6 collective-permute-start.3
  19.2 4.1 collective-permute-done.3.refs_9_.refs_18_.refs_27_
  23.3 1.5 collective-permute-start.4
  24.8 3.0 take.7
  27.8 6.1 %take.8 = (f32[32,128,1,128]{3,2,1,0:T(1,128)S(1)}, f32[32,128,1,128]{3,2,1,0:T(1,128)S(1)}, f32[32,128,1,128]{3,2,1,0:T(1,128)S(1)}, f32[32,128,1,128]{3,2,1,0:T(1,128)S(1)}) custom-call(f32[32,128,4,1,128]{4,3,2,1,0:T(1,128)S(1)} %bitcast.74), custom_call_target="tpu_custom_call" | custom-call | flops 20000000 | bytes 4194304 | tf_op jit(solution)/shard_map/take/pallas_call | solution.py:34
  34.0 6.3 %take.9 = (f32[32,128,1,128]{3,2,1,0:T(1,128)S(1)}, f32[32,128,1,128]{3,2,1,0:T(1,128)S(1)}, f32[32,128,1,128]{3,2,1,0:T(1,128)S(1)}, f32[32,128,1,128]{3,2,1,0:T(1,128)S(1)}) custom-call(f32[32,128,4,1,128]{4,3,2,1,0:T(1,128)S(1)} %bitcast.77), custom_call_target="tpu_custom_call" | custom-call | flops 20000000 | bytes 4194304 | tf_op jit(solution)/shard_map/take/pallas_call | solution.py:34
  40.3 62.2 %collective-permute-done.1.refs_7_.refs_16_.refs_25_ = f32[4,128,128]{2,1,0:T(8,128)S(1)} collective-permute-done((f32[4,128,128]{2,1,0:T(8,128)S(1)}, f32[4,128,128]{2,1,0:T(8,128)S(1)}, u32[]{:S(2)}, u32[]{:S(2)}) %collective-permute-start.1) | collective-permute-done | bytes 262176 | tf_op jit(solution)/shard_map/ppermute | solution.py:15
  102.5 4.0 collective-permute-done.2.refs_8_.refs_17_.refs_26_
  106.5 5.0 %grow.8 = (f32[32,128,128]{2,1,0:T(8,128)S(1)}, f32[32,128,128]{2,1,0:T(8,128)S(1)}, f32[32,128,128]{2,1,0:T(8,128)S(1)}, f32[3,128,128]{2,1,0:T(8,128)S(1)}, f3...) custom-call(f32[32,128,128]{2,1,0:T(8,128)S(1)} %bitcast.66, ...), custom_call_target="tpu_custom_call" | custom-call | flops 30000000 | bytes 12582912 | tf_op jit(solution)/shard_map/grow/pallas_call | solution.py:163
  111.6 2.1 collective-permute-start.11
  113.7 1.9 grow.9
  115.7 1.5 collective-permute-start.7
  117.2 3.6 collective-permute-start.10
  122.3 4.5 collective-permute-done.9.refs_9_.refs_18_.refs_27_
  126.8 82.8 %collective-permute-done.7.refs_7_.refs_16_.refs_25_ = f32[4,128,128]{2,1,0:T(8,128)S(1)} collective-permute-done((f32[4,128,128]{2,1,0:T(8,128)S(1)}, f32[4,128,128]{2,1,0:T(8,128)S(1)}, u32[]{:S(2)}, u32[]{:S(2)}) %collective-permute-start.7) | collective-permute-done | bytes 262176 | tf_op jit(solution)/shard_map/ppermute | solution.py:15
  209.7 2.1 collective-permute-done.8.refs_8_.refs_17_.refs_26_
  211.7 5.0 %grow.10 = (f32[32,128,128]{2,1,0:T(8,128)S(1)}, f32[32,128,128]{2,1,0:T(8,128)S(1)}, f32[32,128,128]{2,1,0:T(8,128)S(1)}, f32[3,128,128]{2,1,0:T(8,128)S(1)}, f...) custom-call(f32[32,128,128]{2,1,0:T(8,128)S(1)} %get-tuple-element.81.refs_0_.refs_3_.refs_4_, ...), custom_call_target="tpu_custom_call" | custom-call | flops 30000000 | bytes 12582912 | tf_op jit(solution)/shard_map/grow/pallas_call | solution.py:163
  216.9 1.9 grow.11
  218.8 3.6 collective-permute-start.17
  222.4 2.5 collective-permute-start.13
  224.9 1.6 collective-permute-start.15
  226.5 4.1 collective-permute-done.15.refs_9_.refs_18_.refs_27_
  232.0 1.9 collective-permute-done.16.refs_10_.refs_19_.refs_28_
  234.0 78.3 %collective-permute-done.13.refs_7_.refs_16_.refs_25_ = f32[4,128,128]{2,1,0:T(8,128)S(1)} collective-permute-done((f32[4,128,128]{2,1,0:T(8,128)S(1)}, f32[4,128,128]{2,1,0:T(8,128)S(1)}, u32[]{:S(2)}, u32[]{:S(2)}) %collective-permute-start.13) | collective-permute-done | bytes 262176 | tf_op jit(solution)/shard_map/ppermute | solution.py:15
  312.3 2.7 collective-permute-done.14.refs_8_.refs_17_.refs_26_
  315.0 5.0 %grow.12 = (f32[32,128,128]{2,1,0:T(8,128)S(1)}, f32[32,128,128]{2,1,0:T(8,128)S(1)}, f32[32,128,128]{2,1,0:T(8,128)S(1)}, f32[3,128,128]{2,1,0:T(8,128)S(1)}, f...) custom-call(f32[32,128,128]{2,1,0:T(8,128)S(1)} %get-tuple-element.92.refs_0_.refs_3_.refs_4_, ...), custom_call_target="tpu_custom_call" | custom-call | flops 30000000 | bytes 12582912 | tf_op jit(solution)/shard_map/grow/pallas_call | solution.py:163
  320.0 3.0 collective-permute-start.23
  323.0 1.9 grow.13
  325.0 2.6 collective-permute-start.19
  327.6 1.8 collective-permute-start.21
  329.3 3.8 collective-permute-done.21.refs_9_.refs_18_.refs_27_
  333.1 1.8 collective-permute-start.22
  334.9 1.7 collective-permute-done.22.refs_10_.refs_19_.refs_28_
  336.5 82.2 %collective-permute-done.19.refs_7_.refs_16_.refs_25_ = f32[4,128,128]{2,1,0:T(8,128)S(1)} collective-permute-done((f32[4,128,128]{2,1,0:T(8,128)S(1)}, f32[4,128,128]{2,1,0:T(8,128)S(1)}, u32[]{:S(2)}, u32[]{:S(2)}) %collective-permute-start.19) | collective-permute-done | bytes 262176 | tf_op jit(solution)/shard_map/ppermute | solution.py:15
  418.7 3.3 collective-permute-done.20.refs_8_.refs_17_.refs_26_
  422.0 8.0 %grow.15 = (f32[32,128,128]{2,1,0:T(8,128)S(1)}, f32[32,128,128]{2,1,0:T(8,128)S(1)}, f32[32,128,128]{2,1,0:T(8,128)S(1)}, f32[6,32,128]{2,1,0:T(8,128)S(1)}) custom-call(f32[32,128,128]{2,1,0:T(8,128)S(1)} %get-tuple-element.105.refs_0_.refs_3_.refs_4_, f32[32,128,128]{2,1,0:T(8,128)S(1)} %get-tuple-element.112.refs_1_.refs_12_.refs_13_, ...), custom_call_target="tpu_custom_call" | custom-call | flops 30000000 | bytes 12582912 | tf_op jit(solution)/shard_map/grow/pallas_call | solution.py:163
  430.0 1.8 collective-permute-start.27
  431.8 2.2 collective-permute-start.28
  435.3 2.7 grow.14
  438.8 1.9 collective-permute-start.25
  442.6 3.7 collective-permute-done.26.refs_7_
  446.3 6.5 %finish.1 = (f32[32,512,128]{2,1,0:T(8,128)}, f32[32,512,128]{2,1,0:T(8,128)}) custom-call(f32[32,128,128]{2,1,0:T(8,128)S(1)} %get-tuple-element.111.refs_0_, f32[32,128,128]{2,1,0:T(8,128)S(1)} %get-tuple-element.113.refs_1_, f32[32,128,128]{2,1,0:T(8,128)S(1)} %get-tuple-element.114.refs_2_, f32[32,128,128]{2,1,0:T(8,128)S(1)} %get-tuple-element.115.refs_3_, ...), custom_call_target="tpu_custom_call" | custom-call | flops 40000000 | bytes 25165824 | tf_op jit(solution)/shard_map/finish/pallas_call | solution.py:213
  (40 shorter events, 7.1 us)
Async XLA Ops:
  0.6 3.4 copy-start
  4.0 3.6 copy-start.1
  5.5 101.0 %collective-permute-start = (f32[32,128,128]{2,1,0:T(8,128)S(1)}, f32[32,128,128]{2,1,0:T(8,128)S(1)}, u32[]{:S(2)}, u32[]{:S(2)}) collective-permute-start(f32[32,128,128]{2,1,0:T(8,128)S(1)} %bitcast.24), channel_id=1, source_target_pairs={{0,1},{1,2},{2,3},{3,4},{4,5},{5,6},{6,7},{7,0},{8,9},{9,10},{10,1... | collective-permute-start | bytes 6291464 | tf_op jit(solution)/shard_map/ppermute | solution.py:15
  7.6 20.2 %slice-start = ((s8[8388608]{0:T(1024)(128)(4,1)}), s8[4194304]{0:T(1024)(128)(4,1)S(1)}, s32[]{:S(2)}) async-start(s8[8388608]{0:T(1024)(128)(4,1)} %bitcast.72), calls=%async_computation | async-start | bytes 8388608
  7.6 26.3 %slice-start.2 = ((s8[8388608]{0:T(1024)(128)(4,1)}), s8[4194304]{0:T(1024)(128)(4,1)S(1)}, s32[]{:S(2)}) async-start(s8[8388608]{0:T(1024)(128)(4,1)} %bitcast.75), calls=%async_computation.2 | async-start | bytes 8388608
  10.0 103.7 %collective-permute-start.5 = (f32[32,128,128]{2,1,0:T(8,128)S(1)}, f32[32,128,128]{2,1,0:T(8,128)S(1)}, u32[]{:S(2)}, u32[]{:S(2)}) collective-permute-start(f32[32,128,128]{2,1,0:T(8,128)S(1)} %bitcast.65), channel_id=1, source_target_pairs={{0,7},{1,0},{2,1},{3,2},{4,3},{5,4},{6,5},{7,6},{8,15},{9,8},{10,9... | collective-permute-start | bytes 6291464 | tf_op jit(solution)/shard_map/ppermute | solution.py:15
  14.3 88.2 %collective-permute-start.1 = (f32[4,128,128]{2,1,0:T(8,128)S(1)}, f32[4,128,128]{2,1,0:T(8,128)S(1)}, u32[]{:S(2)}, u32[]{:S(2)}) collective-permute-start(f32[4,128,128]{2,1,0:T(8,128)S(1)} %bitcast.79), channel_id=1, source_target_pairs={{0,32},{32,64},{64,96},{96,0},{1,33},{33,65},{65,97},{97,1},{2,34}... | collective-permute-start | bytes 786440 | tf_op jit(solution)/shard_map/ppermute | solution.py:15
  17.6 10.2 %slice-start.1 = ((s8[8388608]{0:T(1024)(128)(4,1)}), s8[4194304]{0:T(1024)(128)(4,1)S(1)}, s32[]{:S(2)}) async-start(s8[8388608]{0:T(1024)(128)(4,1)} %bitcast.72), calls=%async_computation.1 | async-start | bytes 8388608
  17.6 89.0 %collective-permute-start.2 = (f32[4,128,128]{2,1,0:T(8,128)S(1)}, f32[4,128,128]{2,1,0:T(8,128)S(1)}, u32[]{:S(2)}, u32[]{:S(2)}) collective-permute-start(f32[4,128,128]{2,1,0:T(8,128)S(1)} %bitcast.78), channel_id=1, source_target_pairs={{0,96},{32,0},{64,32},{96,64},{1,97},{33,1},{65,33},{97,65},{2,98}... | collective-permute-start | bytes 786440 | tf_op jit(solution)/shard_map/ppermute | solution.py:15
  17.6 5.7 %collective-permute-start.3 = (f32[4,32,128]{2,1,0:T(8,128)S(1)}, f32[4,32,128]{2,1,0:T(8,128)S(1)}, u32[]{:S(2)}, u32[]{:S(2)}) collective-permute-start(f32[4,32,128]{2,1,0:T(8,128)S(1)} %bitcast.81), channel_id=1, source_target_pairs={{0,8},{8,16},{16,24},{24,0},{1,9},{9,17},{17,25},{25,1},{2,10},{10... | collective-permute-start | bytes 196616 | tf_op jit(solution)/shard_map/ppermute | solution.py:15
  23.3 10.7 %slice-start.3 = ((s8[8388608]{0:T(1024)(128)(4,1)}), s8[4194304]{0:T(1024)(128)(4,1)S(1)}, s32[]{:S(2)}) async-start(s8[8388608]{0:T(1024)(128)(4,1)} %bitcast.75), calls=%async_computation.3 | async-start | bytes 8388608
  23.3 17.0 %collective-permute-start.4 = (f32[4,32,128]{2,1,0:T(8,128)S(1)}, f32[4,32,128]{2,1,0:T(8,128)S(1)}, u32[]{:S(2)}, u32[]{:S(2)}) collective-permute-start(f32[4,32,128]{2,1,0:T(8,128)S(1)} %bitcast.80), channel_id=1, source_target_pairs={{0,24},{8,0},{16,8},{24,16},{1,25},{9,1},{17,9},{25,17},{2,26},{10... | collective-permute-start | bytes 196616 | tf_op jit(solution)/shard_map/ppermute | solution.py:15
  111.6 100.2 %collective-permute-start.11 = (f32[32,128,128]{2,1,0:T(8,128)S(1)}, f32[32,128,128]{2,1,0:T(8,128)S(1)}, u32[]{:S(2)}, u32[]{:S(2)}) collective-permute-start(f32[32,128,128]{2,1,0:T(8,128)S(1)} %get-tuple-element.74.refs_20_.refs_0_.refs_3_.refs_4_), channel_id=1, source_target_pairs={{0,7},{1,0},{2,1},{3,2},{4,3},{5,4},{6,5},{7,6},{8,15},{9,8},{10,9... | collective-permute-start | bytes 6291464 | tf_op jit(solution)/shard_map/ppermute | solution.py:15
  115.6 101.3 %collective-permute-start.6 = (f32[32,128,128]{2,1,0:T(8,128)S(1)}, f32[32,128,128]{2,1,0:T(8,128)S(1)}, u32[]{:S(2)}, u32[]{:S(2)}) collective-permute-start(f32[32,128,128]{2,1,0:T(8,128)S(1)} %get-tuple-element.81.refs_0_.refs_3_.refs_4_), channel_id=1, source_target_pairs={{0,1},{1,2},{2,3},{3,4},{4,5},{5,6},{6,7},{7,0},{8,9},{9,10},{10,1... | collective-permute-start | bytes 6291464 | tf_op jit(solution)/shard_map/ppermute | solution.py:15
  115.7 94.0 %collective-permute-start.7 = (f32[4,128,128]{2,1,0:T(8,128)S(1)}, f32[4,128,128]{2,1,0:T(8,128)S(1)}, u32[]{:S(2)}, u32[]{:S(2)}) collective-permute-start(f32[4,128,128]{2,1,0:T(8,128)S(1)} %get-tuple-element.83), channel_id=1, source_target_pairs={{0,32},{32,64},{64,96},{96,0},{1,33},{33,65},{65,97},{97,1},{2,34}... | collective-permute-start | bytes 786440 | tf_op jit(solution)/shard_map/ppermute | solution.py:15
  117.2 94.5 %collective-permute-start.8 = (f32[4,128,128]{2,1,0:T(8,128)S(1)}, f32[4,128,128]{2,1,0:T(8,128)S(1)}, u32[]{:S(2)}, u32[]{:S(2)}) collective-permute-start(f32[4,128,128]{2,1,0:T(8,128)S(1)} %get-tuple-element.84), channel_id=1, source_target_pairs={{0,96},{32,0},{64,32},{96,64},{1,97},{33,1},{65,33},{97,65},{2,98}... | collective-permute-start | bytes 786440 | tf_op jit(solution)/shard_map/ppermute | solution.py:15
  117.2 5.0 %collective-permute-start.10 = (f32[4,32,128]{2,1,0:T(8,128)S(1)}, f32[4,32,128]{2,1,0:T(8,128)S(1)}, u32[]{:S(2)}, u32[]{:S(2)}) collective-permute-start(f32[4,32,128]{2,1,0:T(8,128)S(1)} %get-tuple-element.86), channel_id=1, source_target_pairs={{0,24},{8,0},{16,8},{24,16},{1,25},{9,1},{17,9},{25,17},{2,26},{10... | collective-permute-start | bytes 196616 | tf_op jit(solution)/shard_map/ppermute | solution.py:15
  122.2 4.6 %collective-permute-start.9 = (f32[4,32,128]{2,1,0:T(8,128)S(1)}, f32[4,32,128]{2,1,0:T(8,128)S(1)}, u32[]{:S(2)}, u32[]{:S(2)}) collective-permute-start(f32[4,32,128]{2,1,0:T(8,128)S(1)} %get-tuple-element.85), channel_id=1, source_target_pairs={{0,8},{8,16},{16,24},{24,0},{1,9},{9,17},{17,25},{25,1},{2,10},{10... | collective-permute-start | bytes 196616 | tf_op jit(solution)/shard_map/ppermute | solution.py:15
  216.8 98.2 %collective-permute-start.12 = (f32[32,128,128]{2,1,0:T(8,128)S(1)}, f32[32,128,128]{2,1,0:T(8,128)S(1)}, u32[]{:S(2)}, u32[]{:S(2)}) collective-permute-start(f32[32,128,128]{2,1,0:T(8,128)S(1)} %get-tuple-element.93.refs_20_.refs_0_.refs_3_.refs_4_), channel_id=1, source_target_pairs={{0,1},{1,2},{2,3},{3,4},{4,5},{5,6},{6,7},{7,0},{8,9},{9,10},{10,1... | collective-permute-start | bytes 6291464 | tf_op jit(solution)/shard_map/ppermute | solution.py:15
  218.8 104.2 %collective-permute-start.17 = (f32[32,128,128]{2,1,0:T(8,128)S(1)}, f32[32,128,128]{2,1,0:T(8,128)S(1)}, u32[]{:S(2)}, u32[]{:S(2)}) collective-permute-start(f32[32,128,128]{2,1,0:T(8,128)S(1)} %get-tuple-element.92.refs_0_.refs_3_.refs_4_), channel_id=1, source_target_pairs={{0,7},{1,0},{2,1},{3,2},{4,3},{5,4},{6,5},{7,6},{8,15},{9,8},{10,9... | collective-permute-start | bytes 6291464 | tf_op jit(solution)/shard_map/ppermute | solution.py:15
  222.4 89.9 %collective-permute-start.13 = (f32[4,128,128]{2,1,0:T(8,128)S(1)}, f32[4,128,128]{2,1,0:T(8,128)S(1)}, u32[]{:S(2)}, u32[]{:S(2)}) collective-permute-start(f32[4,128,128]{2,1,0:T(8,128)S(1)} %get-tuple-element.95), channel_id=1, source_target_pairs={{0,32},{32,64},{64,96},{96,0},{1,33},{33,65},{65,97},{97,1},{2,34}... | collective-permute-start | bytes 786440 | tf_op jit(solution)/shard_map/ppermute | solution.py:15
  224.9 90.1 %collective-permute-start.14 = (f32[4,128,128]{2,1,0:T(8,128)S(1)}, f32[4,128,128]{2,1,0:T(8,128)S(1)}, u32[]{:S(2)}, u32[]{:S(2)}) collective-permute-start(f32[4,128,128]{2,1,0:T(8,128)S(1)} %get-tuple-element.96), channel_id=1, source_target_pairs={{0,96},{32,0},{64,32},{96,64},{1,97},{33,1},{65,33},{97,65},{2,98}... | collective-permute-start | bytes 786440 | tf_op jit(solution)/shard_map/ppermute | solution.py:15
  224.9 5.7 %collective-permute-start.15 = (f32[4,32,128]{2,1,0:T(8,128)S(1)}, f32[4,32,128]{2,1,0:T(8,128)S(1)}, u32[]{:S(2)}, u32[]{:S(2)}) collective-permute-start(f32[4,32,128]{2,1,0:T(8,128)S(1)} %get-tuple-element.97), channel_id=1, source_target_pairs={{0,8},{8,16},{16,24},{24,0},{1,9},{9,17},{17,25},{25,1},{2,10},{10... | collective-permute-start | bytes 196616 | tf_op jit(solution)/shard_map/ppermute | solution.py:15
  230.6 3.4 collective-permute-start.16
  320.0 102.0 %collective-permute-start.23 = (f32[32,128,128]{2,1,0:T(8,128)S(1)}, f32[32,128,128]{2,1,0:T(8,128)S(1)}, u32[]{:S(2)}, u32[]{:S(2)}) collective-permute-start(f32[32,128,128]{2,1,0:T(8,128)S(1)} %get-tuple-element.100.refs_0_.refs_3_.refs_4_.refs_20_), channel_id=1, source_target_pairs={{0,7},{1,0},{2,1},{3,2},{4,3},{5,4},{6,5},{7,6},{8,15},{9,8},{10,9... | collective-permute-start | bytes 6291464 | tf_op jit(solution)/shard_map/ppermute | solution.py:15
  324.9 110.4 %collective-permute-start.18 = (f32[32,128,128]{2,1,0:T(8,128)S(1)}, f32[32,128,128]{2,1,0:T(8,128)S(1)}, u32[]{:S(2)}, u32[]{:S(2)}) collective-permute-start(f32[32,128,128]{2,1,0:T(8,128)S(1)} %get-tuple-element.105.refs_0_.refs_3_.refs_4_), channel_id=1, source_target_pairs={{0,1},{1,2},{2,3},{3,4},{4,5},{5,6},{6,7},{7,0},{8,9},{9,10},{10,1... | collective-permute-start | bytes 6291464 | tf_op jit(solution)/shard_map/ppermute | solution.py:15
  325.0 93.7 %collective-permute-start.19 = (f32[4,128,128]{2,1,0:T(8,128)S(1)}, f32[4,128,128]{2,1,0:T(8,128)S(1)}, u32[]{:S(2)}, u32[]{:S(2)}) collective-permute-start(f32[4,128,128]{2,1,0:T(8,128)S(1)} %get-tuple-element.107), channel_id=1, source_target_pairs={{0,32},{32,64},{64,96},{96,0},{1,33},{33,65},{65,97},{97,1},{2,34}... | collective-permute-start | bytes 786440 | tf_op jit(solution)/shard_map/ppermute | solution.py:15
  327.6 94.4 %collective-permute-start.20 = (f32[4,128,128]{2,1,0:T(8,128)S(1)}, f32[4,128,128]{2,1,0:T(8,128)S(1)}, u32[]{:S(2)}, u32[]{:S(2)}) collective-permute-start(f32[4,128,128]{2,1,0:T(8,128)S(1)} %get-tuple-element.108), channel_id=1, source_target_pairs={{0,96},{32,0},{64,32},{96,64},{1,97},{33,1},{65,33},{97,65},{2,98}... | collective-permute-start | bytes 786440 | tf_op jit(solution)/shard_map/ppermute | solution.py:15
  327.6 5.5 %collective-permute-start.21 = (f32[4,32,128]{2,1,0:T(8,128)S(1)}, f32[4,32,128]{2,1,0:T(8,128)S(1)}, u32[]{:S(2)}, u32[]{:S(2)}) collective-permute-start(f32[4,32,128]{2,1,0:T(8,128)S(1)} %get-tuple-element.109), channel_id=1, source_target_pairs={{0,8},{8,16},{16,24},{24,0},{1,9},{9,17},{17,25},{25,1},{2,10},{10... | collective-permute-start | bytes 196616 | tf_op jit(solution)/shard_map/ppermute | solution.py:15
  333.1 3.4 collective-permute-start.22
  430.0 16.3 %collective-permute-start.27 = (f32[6,32,128]{2,1,0:T(8,128)S(1)}, f32[6,32,128]{2,1,0:T(8,128)S(1)}, u32[]{:S(2)}, u32[]{:S(2)}) collective-permute-start(f32[6,32,128]{2,1,0:T(8,128)S(1)} %get-tuple-element.117.refs_8_), channel_id=1, source_target_pairs={{0,8},{8,16},{16,24},{24,0},{1,9},{9,17},{17,25},{25,1},{2,10},{10... | collective-permute-start | bytes 294920 | tf_op jit(solution)/shard_map/ppermute | solution.py:15
  431.8 14.5 %collective-permute-start.28 = (f32[6,32,128]{2,1,0:T(8,128)S(1)}, f32[6,32,128]{2,1,0:T(8,128)S(1)}, u32[]{:S(2)}, u32[]{:S(2)}) collective-permute-start(f32[6,32,128]{2,1,0:T(8,128)S(1)} %get-tuple-element.117.refs_8_), channel_id=1, source_target_pairs={{0,24},{8,0},{16,8},{24,16},{1,25},{9,1},{17,9},{25,17},{2,26},{10... | collective-permute-start | bytes 294920 | tf_op jit(solution)/shard_map/ppermute | solution.py:15
  434.0 12.3 %collective-permute-start.29 = (f32[6,32,128]{2,1,0:T(8,128)S(1)}, f32[6,32,128]{2,1,0:T(8,128)S(1)}, u32[]{:S(2)}, u32[]{:S(2)}) collective-permute-start(f32[6,32,128]{2,1,0:T(8,128)S(1)} %get-tuple-element.117.refs_8_), channel_id=1, source_target_pairs={{0,16},{8,24},{16,0},{24,8},{1,17},{9,25},{17,1},{25,9},{2,18},{10... | collective-permute-start | bytes 294920 | tf_op jit(solution)/shard_map/ppermute | solution.py:15
  438.0 4.0 collective-permute-start.24
  438.8 3.8 collective-permute-start.25
  442.0 4.3 collective-permute-start.26
